TPU v7x, 16 devices: a whole 2x2x2 slice. The times are simulated.
16 devices in a mesh: dp: 4 (over z, y), cp: 4 (over x, core).
Axes of the slice: x: 2, y: 2, z: 2, core: 2. Of those that a mesh axis runs over, the one named last changes fastest.
Arguments:
- x_in: bfloat16 [4, 2048, 1536], P('dp', 'cp'), parts along dimension 0
- ln_w: bfloat16 [1536], replicated
- ln_b: bfloat16 [1536], replicated
- w_q: bfloat16 [1536, 1536], replicated
- b_q: bfloat16 [1536], replicated
- w_k: bfloat16 [1536, 256], replicated
- b_k: bfloat16 [256], replicated
- w_v: bfloat16 [1536, 256], replicated
- b_v: bfloat16 [256], replicated
- w_o: bfloat16 [1536, 1536], replicated
- b_o: bfloat16 [1536], replicated
- long_factor: float32 [64], replicated
- dy_out: bfloat16 [4, 2048, 1536], P('dp', 'cp'), parts along dimension 0
Outputs:
- output 1: bfloat16 [4, 2048, 1536], P('dp', 'cp'), parts along dimension 0
- output 2: bfloat16 [4, 2048, 1536], P('dp', 'cp'), parts along dimension 0
- output 3: float32 [6144, 1536], P(('dp', 'cp')), parts along dimension 0
- output 4: float32 [6144, 256], P(('dp', 'cp')), parts along dimension 0
- output 5: float32 [6144, 256], P(('dp', 'cp')), parts along dimension 0
- output 6: float32 [6144, 1536], P(('dp', 'cp')), parts along dimension 0
- output 7: float32 [6144], P('dp'), parts along dimension 0
- output 8: float32 [6144], P('dp'), parts along dimension 0
- output 9: float32 [6144], P('dp'), parts along dimension 0
- output 10: float32 [1024], P('dp'), parts along dimension 0
- output 11: float32 [1024], P('dp'), parts along dimension 0
- output 12: float32 [6144], P('dp'), parts along dimension 0
There are 4 independent parts. A program takes and returns all parts, laid end to end along the dimension named above; an argument that names none is the same for every part.
All inputs are finite; a program needn't handle non-finite values.
Results may differ from a plain program's by a relative error of at most 0.02.
Values are sent between devices in bfloat16 or wider.
A program may use at most 1 GiB of HBM per device.

v0:
```python
import math
import jax
import jax.numpy as jnp
from jax import lax
from jax.sharding import PartitionSpec as P

EPS = 1e-5
THETA = 10000.0
ROPE_SCALE = math.sqrt(1.0 + math.log(32.0) / math.log(4096.0))


def block_positions(block, piece, groups):
    offsets = jnp.arange(piece, dtype=jnp.int32)
    return jnp.concatenate([block * piece + offsets, (2 * groups - 1 - block) * piece + offsets])


def sequence_positions(piece, groups):
    block_ids = jnp.arange(groups, dtype=jnp.int32)[:, None]
    offsets = jnp.arange(piece, dtype=jnp.int32)[None, :]
    both = jnp.concatenate([block_ids * piece + offsets, (2 * groups - 1 - block_ids) * piece + offsets], axis=1)
    return both.reshape(2 * groups * piece)


def rope_tables(positions, long_factor):
    half_dim = long_factor.shape[0]
    exponent = jnp.arange(half_dim, dtype=jnp.float32) * (1.0 / half_dim)
    inv_freq = 1.0 / (long_factor * THETA ** exponent)
    angle = positions.astype(jnp.float32)[:, None] * inv_freq[None, :]
    return (jnp.cos(angle) * ROPE_SCALE)[:, None, :], (jnp.sin(angle) * ROPE_SCALE)[:, None, :]


def rope_apply(tensor, cos_t, sin_t):
    half_dim = tensor.shape[-1] // 2
    first = tensor[..., :half_dim]
    second = tensor[..., half_dim:]
    return jnp.concatenate([first * cos_t - second * sin_t, second * cos_t + first * sin_t], axis=-1)


def rope_transpose(grads, cos_t, sin_t):
    half_dim = grads.shape[-1] // 2
    first = grads[..., :half_dim]
    second = grads[..., half_dim:]
    return jnp.concatenate([first * cos_t + second * sin_t, second * cos_t - first * sin_t], axis=-1)


def solution(mesh):
    groups = mesh.shape['cp']
    row_spec = P('dp', 'cp', None)
    mat_spec = P(('dp', 'cp'), None)
    vec_spec = P('dp')

    def device_fn(x_in, ln_w, ln_b, w_q, b_q, w_k, b_k, w_v, b_v, w_o, b_o, long_factor, dy_out):
        rank = lax.axis_index('cp')
        x_rows = x_in[0]
        tokens = x_rows.shape[0]
        piece = tokens // 2
        head_dim = 2 * long_factor.shape[0]
        heads = w_q.shape[1] // head_dim
        kv_heads = w_k.shape[1] // head_dim
        group_size = heads // kv_heads
        scale = head_dim ** -0.5
        x_f = x_rows.astype(jnp.float32)
        centered = x_f - jnp.mean(x_f, axis=-1, keepdims=True)
        inv_std = lax.rsqrt(jnp.mean(centered * centered, axis=-1, keepdims=True) + EPS)
        x_hat = centered * inv_std
        gain = ln_w.astype(jnp.float32)
        hidden = (x_hat * gain + ln_b.astype(jnp.float32)).astype(jnp.bfloat16)
        q_proj = (jnp.dot(hidden, w_q, preferred_element_type=jnp.float32) + b_q.astype(jnp.float32)).astype(jnp.bfloat16)
        k_proj = (jnp.dot(hidden, w_k, preferred_element_type=jnp.float32) + b_k.astype(jnp.float32)).astype(jnp.bfloat16)
        v_proj = (jnp.dot(hidden, w_v, preferred_element_type=jnp.float32) + b_v.astype(jnp.float32)).astype(jnp.bfloat16)
        pos_local = block_positions(rank, piece, groups)
        cos_t, sin_t = rope_tables(pos_local, long_factor)
        q_rot = rope_apply(q_proj.astype(jnp.float32).reshape(tokens, heads, head_dim), cos_t, sin_t).astype(jnp.bfloat16)
        k_rot = rope_apply(k_proj.astype(jnp.float32).reshape(tokens, kv_heads, head_dim), cos_t, sin_t).astype(jnp.bfloat16)
        v_heads = v_proj.reshape(tokens, kv_heads, head_dim)

        kv_all = lax.all_gather(jnp.stack([k_rot, v_heads]), 'cp', axis=1, tiled=True)
        k_all = kv_all[0]
        v_all = kv_all[1]
        visible = (sequence_positions(piece, groups)[None, :] <= pos_local[:, None])[:, None, None, :]
        q_groups = q_rot.reshape(tokens, kv_heads, group_size, head_dim)
        scores = jnp.einsum('tkgd,skd->tkgs', q_groups, k_all, preferred_element_type=jnp.float32) * scale
        probs = jax.nn.softmax(jnp.where(visible, scores, -1e30), axis=-1)
        probs_b = probs.astype(jnp.bfloat16)
        attn_rows = jnp.einsum('tkgs,skd->tkgd', probs_b, v_all, preferred_element_type=jnp.float32).astype(jnp.bfloat16).reshape(tokens, heads * head_dim)
        z_out = jnp.dot(attn_rows, w_o, preferred_element_type=jnp.float32) + b_o.astype(jnp.float32)
        y_rows = (x_f + z_out).astype(jnp.bfloat16)

        d_rows = dy_out[0]
        d_bo = jnp.sum(d_rows.astype(jnp.float32), axis=0)
        d_wo = jnp.einsum('tc,td->cd', attn_rows, d_rows, preferred_element_type=jnp.float32)
        d_attn = jnp.einsum('td,cd->tc', d_rows, w_o, preferred_element_type=jnp.float32).astype(jnp.bfloat16).reshape(tokens, kv_heads, group_size, head_dim)
        d_probs = jnp.einsum('tkgd,skd->tkgs', d_attn, v_all, preferred_element_type=jnp.float32).astype(jnp.bfloat16).astype(jnp.float32)
        row_dot = jnp.sum(probs * d_probs, axis=-1, keepdims=True)
        d_scores = (probs * (d_probs - row_dot) * scale).astype(jnp.bfloat16)
        d_kv_all = jnp.stack([
            jnp.einsum('tkgs,tkgd->skd', d_scores, q_groups, preferred_element_type=jnp.float32),
            jnp.einsum('tkgs,tkgd->skd', probs_b, d_attn, preferred_element_type=jnp.float32)])
        d_q_rot = jnp.einsum('tkgs,skd->tkgd', d_scores, k_all, preferred_element_type=jnp.float32).astype(jnp.bfloat16)
        d_kv = lax.psum_scatter(d_kv_all, 'cp', scatter_dimension=1, tiled=True)

        d_q = rope_transpose(d_q_rot.astype(jnp.float32).reshape(tokens, heads, head_dim), cos_t, sin_t).astype(jnp.bfloat16).reshape(tokens, heads * head_dim)
        d_k = rope_transpose(d_kv[0].astype(jnp.bfloat16).astype(jnp.float32), cos_t, sin_t).astype(jnp.bfloat16).reshape(tokens, kv_heads * head_dim)
        d_v = d_kv[1].astype(jnp.bfloat16).reshape(tokens, kv_heads * head_dim)
        d_wq = jnp.einsum('tc,te->ce', hidden, d_q, preferred_element_type=jnp.float32)
        d_wk = jnp.einsum('tc,te->ce', hidden, d_k, preferred_element_type=jnp.float32)
        d_wv = jnp.einsum('tc,te->ce', hidden, d_v, preferred_element_type=jnp.float32)
        d_hidden = (jnp.einsum('te,ce->tc', d_q, w_q, preferred_element_type=jnp.float32)
                    + jnp.einsum('te,ce->tc', d_k, w_k, preferred_element_type=jnp.float32)
                    + jnp.einsum('te,ce->tc', d_v, w_v, preferred_element_type=jnp.float32)).astype(jnp.bfloat16).astype(jnp.float32)
        d_lnw = jnp.sum(d_hidden * x_hat, axis=0)
        d_lnb = jnp.sum(d_hidden, axis=0)
        value_a6 = d_hidden * gain
        d_xln = inv_std * (value_a6 - jnp.mean(value_a6, axis=-1, keepdims=True) - x_hat * jnp.mean(value_a6 * x_hat, axis=-1, keepdims=True))
        dx_rows = (d_rows.astype(jnp.float32) + d_xln).astype(jnp.bfloat16)
        d_bq = jnp.sum(d_q.astype(jnp.float32), axis=0)
        d_bk = jnp.sum(d_k.astype(jnp.float32), axis=0)
        d_bv = jnp.sum(d_v.astype(jnp.float32), axis=0)

        d_mats = tuple(lax.psum_scatter(grad_mat, 'cp', scatter_dimension=0, tiled=True) for grad_mat in (d_wq, d_wk, d_wv, d_wo))
        d_vecs = lax.psum((d_lnw, d_lnb, d_bq, d_bk, d_bv, d_bo), 'cp')
        return (y_rows[None], dx_rows[None]) + d_mats + tuple(d_vecs)

    in_specs = (row_spec,) + (P(),) * 11 + (row_spec,)
    out_specs = (row_spec, row_spec) + (mat_spec,) * 4 + (vec_spec,) * 6
    return jax.shard_map(device_fn, mesh=mesh, in_specs=in_specs, out_specs=out_specs, check_vma=False)
```

profile of v0, /device:TPU:0, one launch (start us, length us, event | category | flops | bytes accessed | tf_op | source)
XLA Modules:
  0.0 428.8 jit_solution(11142073400281975243)
XLA Ops:
  9.4 1.7 convert_reduce_fusion.1
  11.1 2.0 fusion.31
  17.0 2.0 fusion.58
  21.3 7.1 %fusion.41 = f32[512,1536]{1,0:T(8,128)} fusion(bf16[512,1536]{1,0:T(8,128)(2,1)} %copy-done.13, bf16[1536,1536]{1,0:T(8,128)(2,1)} %param.16, f32[1536]{0:T(1024)S(1)} %convert_element_type.183), kind=kOutput, calls=%fused_computation.61 | convolution fusion | flops 2418278400 | bytes 9443328 | tf_op jit(solution)/shard_map/dot_general | solution.py:68
  28.4 3.6 copy.69
  32.0 2.4 subtract_convert_fusion
  34.4 1.5 copy.70
  35.9 1.5 copy.71
  37.4 6.6 %convolution_convert_fusion.1 = bf16[512,1536]{1,0:T(8,128)(2,1)} fusion(bf16[1536,1536]{1,0:T(8,128)(2,1)} %param.22, bf16[1,512,1536]{2,1,0:T(8,128)(2,1)} %param.25), kind=kOutput, calls=%fused_computation.62 | convolution fusion | flops 2416705536 | bytes 7864320 | tf_op jit(solution)/shard_map/td,cd->tc/dot_general | solution.py:92
  44.0 1.7 copy.74
  46.5 26.7 %fusion.75 = (f32[512,2,6]{0,2,1:T(8,128)S(1)}, f32[512,2,6,2048]{0,3,2,1:T(8,128)}) fusion(pred[512,2048]{0,1:T(8,128)(4,1)S(1)} %broadcast_compare_fusion, bf16[2,2048,2,128]{3,1,2,0:T(8,128)(2,1)} %all-gather.2.cloned.1.call-done, bf16[512,2,6,64]{3,0,2,1:T(8,128)(2,1)} %bitcast.208, bf16[512,2,6,64]{3,0,2,1:T(8,128)(2,1)} %bitcast.206), kind=kOutput, calls=%fused_computation.127 | convolution fusion | flops 3274704896 | bytes 55599104 | tf_op jit(solution)/shard_map/sub | solution.py:83
  73.3 19.4 %fusion.45 = f32[1,2048,2,128]{3,1,2,0:T(8,128)} fusion(bf16[512,2,6,128]{0,3,2,1:T(8,128)(2,1)S(1)} %bitcast.199, f32[512,2,6,2048]{0,3,2,1:T(8,128)} %get-tuple-element.45, f32[512,2,6]{0,2,1:T(8,128)S(1)} %get-tuple-element.44), kind=kOutput, calls=%fused_computation.66 | convolution fusion | flops 3246391296 | bytes 54026240 | tf_op jit(solution)/shard_map/tkgs,tkgd->skd/dot_general | solution.py:98
  92.7 12.9 %convolution_convert_fusion = bf16[2,2048,512,6]{2,1,3,0:T(8,128)(2,1)} fusion(bf16[512,2,6,128]{0,3,2,1:T(8,128)(2,1)S(1)} %bitcast.200, bf16[2,2048,2,128]{3,1,2,0:T(8,128)(2,1)} %all-gather.2.cloned.1.call-done), kind=kOutput, calls=%fused_computation.17 | convolution fusion | flops 3233808384 | bytes 27787264 | tf_op jit(solution)/shard_map/tkgd,skd->tkgs/dot_general | solution.py:93
  105.6 50.3 %fusion.43 = f32[1,2048,2,128]{3,1,2,0:T(8,128)} fusion(bf16[2,2048,512,6]{2,1,3,0:T(8,128)(2,1)} %convolution_convert_fusion, bf16[512,2,6,64]{3,0,2,1:T(8,128)(2,1)} %bitcast.209, bf16[512,2,6,64]{3,0,2,1:T(8,128)(2,1)} %bitcast.207, f32[512,2,6,2048]{0,3,2,1:T(8,128)} %get-tuple-element.45, f32[512,2,6]{0,2,1:T(8,128)S(1)} %get-tuple-element.44), kind=kOutput, calls=%fused_computation.64 | convolution fusion | flops 3337625600 | bytes 79192064 | tf_op jit(solution)/shard_map/tkgs,tkgd->skd/dot_general | solution.py:97
  155.9 3.9 pad_maximum_fusion
  159.8 1.3 copy-done.2
  161.1 1.8 fusion.53
  162.9 39.9 %reduce-scatter.6.cloned.1.call-done = f32[2,512,2,128]{3,1,2,0:T(8,128)} async-done(((f32[2,2048,2,128]{3,1,2,0:T(8,128)}), f32[2,512,2,128]{3,1,2,0:T(8,128)}) %reduce-scatter.6.cloned.1.call-update) | async-done | bytes 1048592 | tf_op jit(solution)/shard_map/reduce_scatter | solution.py:100
  204.6 3.2 fusion.78
  209.3 3.2 fusion.79
  212.6 49.3 %fusion.52 = f32[2,128,512,6]{2,1,3,0:T(8,128)} fusion(bf16[2,2048,512,6]{2,1,3,0:T(8,128)(2,1)} %convolution_convert_fusion, bf16[2,2048,2,128]{3,1,2,0:T(8,128)(2,1)} %all-gather.2.cloned.1.call-done, f32[512,2,6,2048]{0,3,2,1:T(8,128)} %get-tuple-element.45, f32[512,2,6]{0,2,1:T(8,128)S(1)} %get-tuple-element.44), kind=kOutput, calls=%fused_computation.70 | convolution fusion | flops 3336052736 | bytes 155254784 | tf_op jit(solution)/shard_map/tkgs,skd->tkgd/dot_general | solution.py:99
  261.9 2.5 multiply_add_fusion
  265.9 5.1 %fusion.77 = f32[1536,1536]{1,0:T(8,128)} fusion(bf16[512,1536]{1,0:T(8,128)(2,1)S(1)} %copy-done.3, bf16[512,1536]{0,1:T(8,128)(2,1)S(1)} %bitcast.204), kind=kOutput, calls=%fused_computation.129 | convolution fusion | flops 2415919104 | bytes 12582912 | tf_op jit(solution)/shard_map/tc,te->ce/dot_general | solution.py:105
  271.4 17.4 %fusion.48 = bf16[2,128,512,6]{2,1,3,0:T(8,128)(2,1)S(1)} fusion(bf16[2,2048,2,128]{3,1,2,0:T(8,128)(2,1)} %all-gather.2.cloned.1.call-done, f32[512,2,6,2048]{0,3,2,1:T(8,128)} %get-tuple-element.45, f32[512,2,6]{0,2,1:T(8,128)S(1)} %get-tuple-element.44), kind=kOutput, calls=%fused_computation.68 | convolution fusion | flops 3247177728 | bytes 52977664 | tf_op jit(solution)/shard_map/tkgs,skd->tkgd/dot_general | solution.py:85
  289.9 5.2 %fusion.55 = f32[1536,1536]{1,0:T(8,128)} fusion(bf16[512,1536]{0,1:T(8,128)(2,1)S(1)} %bitcast.218, bf16[1,512,1536]{2,1,0:T(8,128)(2,1)S(1)} %copy-done.15), kind=kOutput, calls=%fused_computation.74 | convolution fusion | flops 2415919104 | bytes 12582912 | tf_op jit(solution)/shard_map/tc,td->cd/dot_general | solution.py:91
  295.8 5.1 %fusion.76 = f32[512,1536]{1,0:T(8,128)S(1)} fusion(bf16[512,1536]{0,1:T(8,128)(2,1)} %bitcast.205, bf16[1536,1536]{1,0:T(8,128)(2,1)} %param.16), kind=kOutput, calls=%fused_computation.128 | convolution fusion | flops 2415919104 | bytes 9437184 | tf_op jit(solution)/shard_map/te,ce->tc/dot_general | solution.py:108
  301.0 6.1 %fusion.44 = bf16[1,512,1536]{2,1,0:T(8,128)(2,1)} fusion(bf16[512,1536]{0,1:T(8,128)(2,1)S(1)} %bitcast.219, bf16[1536,1536]{1,0:T(8,128)(2,1)} %param.22, bf16[1,512,1536]{2,1,0:T(8,128)(2,1)S(1)} %copy-done.2, f32[1536]{0:T(1024)S(1)} %convert_element_type.188), kind=kOutput, calls=%fused_computation.65 | convolution fusion | flops 2419064832 | bytes 9443328 | tf_op jit(solution)/shard_map/dot_general | solution.py:86
  307.8 1.8 fusion.39
  309.7 2.7 convert_reduce_fusion.2
  312.4 12.9 %all-reduce = (f32[1536]{0:T(1024)}, f32[1536]{0:T(1024)}, f32[1536]{0:T(1024)}, f32[256]{0:T(256)}, f32[256]{0:T(256)}, /*index=5*/f32[1536]{0:T(1024)}) all-reduce(f32[1536]{0:T(1024)S(1)} %get-tuple-element.12, f32[1536]{0:T(1024)S(1)} %get-tuple-element.15, f32[1536]{0:T(1024)S(1)} %bitcast.214, ...), channel_id=1, replica_groups=mesh['dp'=4,'cp'=4] {'cp'}, use_global_device_ids=true, to_apply=%region_13.14 | all-reduce | flops 6656 | bytes 53248 | tf_op jit(solution)/shard_map/psum | solution.py:121
  325.2 20.1 %reduce-scatter.8.cloned.1.call-done = f32[384,1536]{1,0:T(8,128)} async-done(((f32[1536,1536]{1,0:T(8,128)}), f32[384,1536]{1,0:T(8,128)}) %reduce-scatter.8.cloned.1.call-update) | async-done | bytes 2359312 | tf_op jit(solution)/shard_map/reduce_scatter | solution.py:120
  345.3 76.4 %reduce-scatter.14.cloned.1.call-done = f32[384,1536]{1,0:T(8,128)} async-done(((f32[1536,1536]{1,0:T(8,128)}), f32[384,1536]{1,0:T(8,128)}) %reduce-scatter.14.cloned.1.call-update) | async-done | bytes 2359312 | tf_op jit(solution)/shard_map/reduce_scatter | solution.py:120
  (118 shorter events, 16.6 us)
Async XLA Ops:
  7.2 8.7 %copy-start = (bf16[1536,256]{1,0:T(8,128)(2,1)S(1)}, bf16[1536,256]{1,0:T(8,128)(2,1)}, u32[]{:S(2)}) copy-start(bf16[1536,256]{1,0:T(8,128)(2,1)} %param.20) | copy-start | bytes 2359300
  7.2 6.8 %copy-start.1 = (bf16[1,512,1536]{2,1,0:T(8,128)(2,1)S(1)}, bf16[1,512,1536]{2,1,0:T(8,128)(2,1)}, u32[]{:S(2)}) copy-start(bf16[1,512,1536]{2,1,0:T(8,128)(2,1)} %param.13) | copy-start | bytes 4718596
  7.2 5.9 %copy-start.27 = (bf16[1536]{0:T(1024)(128)(2,1)S(1)}, bf16[1536]{0:T(1024)(128)(2,1)}, u32[]{:S(2)}) copy-start(bf16[1536]{0:T(1024)(128)(2,1)} %param.14) | copy-start | bytes 9220
  7.2 5.9 %copy-start.28 = (bf16[1536]{0:T(1024)(128)(2,1)S(1)}, bf16[1536]{0:T(1024)(128)(2,1)}, u32[]{:S(2)}) copy-start(bf16[1536]{0:T(1024)(128)(2,1)} %param.15) | copy-start | bytes 9220
  7.2 39.3 %all-gather.2.cloned.1.call-start = ((), (), s32[]{:S(2)}) async-start(), calls=%async_computation.5 | async-start | bytes 2621440 | tf_op jit(solution)/shard_map/all_gather | solution.py:77
  11.1 5.4 %copy-start.23 = (f32[512]{0:T(512)}, f32[512]{0:T(512)S(1)}, u32[]{:S(2)}) copy-start(f32[512]{0:T(512)S(1)} %broadcast_multiply_fusion.2) | copy-start | bytes 6148
  13.1 3.4 copy-start.25
  13.1 3.4 copy-start.19
  13.2 3.4 copy-start.21
  13.7 18.2 %copy-start.8 = (f32[512,64]{0,1:T(8,128)}, f32[512,64]{0,1:T(8,128)S(1)}, u32[]{:S(2)}) copy-start(f32[512,64]{0,1:T(8,128)S(1)} %get-tuple-element.40) | copy-start | bytes 393220
  13.8 18.2 %copy-start.10 = (f32[512,64]{0,1:T(8,128)}, f32[512,64]{0,1:T(8,128)S(1)}, u32[]{:S(2)}) copy-start(f32[512,64]{0,1:T(8,128)S(1)} %get-tuple-element.41) | copy-start | bytes 393220
  13.9 5.6 %copy-start.4 = (f32[512,64]{1,0:T(8,128)}, f32[512,64]{1,0:T(8,128)S(1)}, u32[]{:S(2)}) copy-start(f32[512,64]{1,0:T(8,128)S(1)} %copy.65) | copy-start | bytes 393220
  14.0 5.5 %copy-start.6 = (f32[512,64]{1,0:T(8,128)}, f32[512,64]{1,0:T(8,128)S(1)}, u32[]{:S(2)}) copy-start(f32[512,64]{1,0:T(8,128)S(1)} %copy.67) | copy-start | bytes 393220
  19.0 2.3 copy-start.29
  20.7 182.2 %reduce-scatter.6.cloned.1.call-start = ((), (), s32[]{:S(2)}) async-start(), calls=%async_computation.6 | async-start | bytes 5242880 | tf_op jit(solution)/shard_map/reduce_scatter | solution.py:100
  105.6 50.3 %copy-start.12 = (f32[1,2048,2,128]{3,1,2,0:T(8,128)S(1)}, f32[1,2048,2,128]{3,1,2,0:T(8,128)}, u32[]{:S(2)}) copy-start(f32[1,2048,2,128]{3,1,2,0:T(8,128)} %fusion.45) | copy-start | bytes 6291460
  159.7 1.4 copy-start.20
  159.7 1.4 copy-start.22
  159.7 1.4 copy-start.24
  159.7 44.2 %copy-start.5 = (f32[512,64]{1,0:T(8,128)S(1)}, f32[512,64]{1,0:T(8,128)}, u32[]{:S(2)}) copy-start(f32[512,64]{1,0:T(8,128)} %copy-done.4) | copy-start | bytes 393220
  159.8 44.2 %copy-start.7 = (f32[512,64]{1,0:T(8,128)S(1)}, f32[512,64]{1,0:T(8,128)}, u32[]{:S(2)}) copy-start(f32[512,64]{1,0:T(8,128)} %copy-done.6) | copy-start | bytes 393220
  159.8 165.4 %reduce-scatter.10.cloned.1.call-start = ((), (), s32[]{:S(2)}) async-start(), calls=%async_computation.8 | async-start | bytes 1966080 | tf_op jit(solution)/shard_map/reduce_scatter | solution.py:120
  207.8 117.5 %reduce-scatter.12.cloned.1.call-start = ((), (), s32[]{:S(2)}) async-start(), calls=%async_computation.9 | async-start | bytes 1966080 | tf_op jit(solution)/shard_map/reduce_scatter | solution.py:120
  212.5 49.4 %copy-start.9 = (f32[512,64]{0,1:T(8,128)S(1)}, f32[512,64]{0,1:T(8,128)}, u32[]{:S(2)}) copy-start(f32[512,64]{0,1:T(8,128)} %copy-done.8) | copy-start | bytes 393220
  212.5 49.4 %copy-start.11 = (f32[512,64]{0,1:T(8,128)S(1)}, f32[512,64]{0,1:T(8,128)}, u32[]{:S(2)}) copy-start(f32[512,64]{0,1:T(8,128)} %copy-done.10) | copy-start | bytes 393220
  212.5 132.8 %reduce-scatter.8.cloned.1.call-start = ((), (), s32[]{:S(2)}) async-start(), calls=%async_computation.7 | async-start | bytes 11796480 | tf_op jit(solution)/shard_map/reduce_scatter | solution.py:120
  261.9 4.0 copy-start.3
  271.0 150.6 %reduce-scatter.14.cloned.1.call-start = ((), (), s32[]{:S(2)}) async-start(), calls=%async_computation.10 | async-start | bytes 11796480 | tf_op jit(solution)/shard_map/reduce_scatter | solution.py:120
  271.3 18.6 %copy-start.15 = (bf16[1,512,1536]{2,1,0:T(8,128)(2,1)S(1)}, bf16[1,512,1536]{2,1,0:T(8,128)(2,1)}, u32[]{:S(2)}) copy-start(bf16[1,512,1536]{2,1,0:T(8,128)(2,1)} %param.25) | copy-start | bytes 4718596
  295.8 5.1 %copy-start.32 = (bf16[2,128,512,6]{2,1,3,0:T(8,128)(2,1)S(1)}, bf16[2,128,512,6]{2,1,3,0:T(8,128)(2,1)}, u32[]{:S(2)}) copy-start(bf16[2,128,512,6]{2,1,3,0:T(8,128)(2,1)} %copy-done.31) | copy-start | bytes 4718596
  301.0 6.2 %copy-start.18 = (bf16[1536,256]{1,0:T(8,128)(2,1)S(1)}, bf16[1536,256]{1,0:T(8,128)(2,1)}, u32[]{:S(2)}) copy-start(bf16[1536,256]{1,0:T(8,128)(2,1)} %param.18) | copy-start | bytes 2359300
  307.8 1.9 copy-start.16
  (7 other events, 8.1 us)
Sparse Core Ops, SparseCore 0:
  20.8 23.2 all-gather.1
  159.9 42.9 reduce-scatter.5
  207.9 24.1 reduce-scatter.9
  235.0 24.1 reduce-scatter.11
  271.2 74.0 reduce-scatter.7
  348.3 73.3 reduce-scatter.13
where the time goes:
time: 433 us; the launch traced here: 429 us
  matrix products  223 us (52%)
  waiting for transfers between devices  137 us (32%)
  other arithmetic  25.1 us (6%)
  local copies, waits for them, and re-layouts  15.3 us (4%)
  between operations  15 us (3%)
  blocking collectives  12.9 us (3%)
    reduce_scatter x4, waiting for transfers between devices, device_fn(): lax.psum_scatter(grad_mat, 'cp', scatter_dimension=0, tiled=True)  96.5 us
    dot_general x1, matrix products, device_fn(): jnp.einsum('tkgs,tkgd->skd', d_scores, q_groups, preferred_element_type=j...  50.3 us
    dot_general x1, matrix products, device_fn(): jnp.einsum('tkgs,skd->tkgd', d_scores, k_all, preferred_element_type=jnp....  49.3 us
    reduce_scatter x1, waiting for transfers between devices, device_fn(): d_kv = lax.psum_scatter(d_kv_all, 'cp', scatter_dimension=1, tiled=True)  39.9 us
    sub x1, matrix products, device_fn(): probs = jax.nn.softmax(jnp.where(visible, scores, -1e+30), axis=-1)  26.7 us
    dot_general x1, matrix products, device_fn(): jnp.einsum('tkgs,tkgd->skd', probs_b, d_attn, preferred_element_type=jnp....  19.4 us
    dot_general x1, matrix products, device_fn(): jnp.einsum('tkgs,skd->tkgd', probs_b, v_all, preferred_element_type=jnp.f...  17.4 us
    dot_general x1, matrix products, device_fn(): jnp.einsum('tkgd,skd->tkgs', d_attn, v_all, preferred_element_type=jnp.fl...  12.9 us
  transfers between devices with their start and end apart: 6, of which 3 were waited for; matrix products, arithmetic and copies ran while one was open for 30% of the time, Pallas kernels for 0%

commit v1 on v0

v1 whole, which is shorter than its diff:
```python
import functools
import math
import jax
import jax.numpy as jnp
from jax import lax
from jax.experimental import pallas as pl
from jax.experimental.pallas import tpu as pltpu
from jax.sharding import PartitionSpec as P

EPS = 1e-5
THETA = 10000.0
ROPE_SCALE = math.sqrt(1.0 + math.log(32.0) / math.log(4096.0))
LOG2E = math.log2(math.e)
NEG = -1e30
F32 = jnp.float32
BF16 = jnp.bfloat16


def dot(a, b):
    return lax.dot_general(a, b, (((1,), (0,)), ((), ())), preferred_element_type=F32)


def dot_nt(a, b):
    return lax.dot_general(a, b, (((1,), (1,)), ((), ())), preferred_element_type=F32)


def dot_tn(a, b):
    return lax.dot_general(a, b, (((0,), (0,)), ((), ())), preferred_element_type=F32)


def rope_tables(positions, long_factor):
    half_dim = long_factor.shape[0]
    exponent = jnp.arange(half_dim, dtype=F32) * (1.0 / half_dim)
    inv_freq = 1.0 / (long_factor * THETA ** exponent)
    angle = positions.astype(F32)[:, None] * inv_freq[None, :]
    cos_t = jnp.cos(angle) * ROPE_SCALE
    sin_t = jnp.sin(angle) * ROPE_SCALE
    return jnp.concatenate([cos_t, cos_t], axis=1), jnp.concatenate([-sin_t, sin_t], axis=1)


def params(n, mib=48):
    return pltpu.CompilerParams(dimension_semantics=("arbitrary",) * n, vmem_limit_bytes=mib << 20)


def ln_body(x_ref, w_ref, b_ref, h_ref):
    x = x_ref[...].astype(F32)
    cen = x - jnp.mean(x, axis=-1, keepdims=True)
    inv = lax.rsqrt(jnp.mean(cen * cen, axis=-1, keepdims=True) + EPS)
    h_ref[...] = (cen * inv * w_ref[...].astype(F32) + b_ref[...].astype(F32)).astype(BF16)


def layer_norm(x, w, b, tm=256):
    rows, width = x.shape
    vec = pl.BlockSpec((1, width), lambda i: (0, 0))
    return pl.pallas_call(
        ln_body,
        grid=(rows // tm,),
        in_specs=[pl.BlockSpec((tm, width), lambda i: (i, 0)), vec, vec],
        out_specs=pl.BlockSpec((tm, width), lambda i: (i, 0)),
        out_shape=jax.ShapeDtypeStruct((rows, width), BF16),
        compiler_params=params(1, 24),
        cost_estimate=pl.CostEstimate(flops=rows * width * 12, bytes_accessed=rows * width * 4, transcendentals=0),
        name="ln_rows",
    )(x, w, b)


def qkv_body(nh, hd, c_ref, h_ref, wq_ref, wk_ref, wv_ref, bq_ref, bk_ref, bv_ref, cos_ref, sin_ref, q_ref, k_ref, v_ref):
    h = h_ref[...]
    cos_t = cos_ref[...]
    sin_t = sin_ref[...]

    def rope(t):
        t = t.astype(BF16).astype(F32)
        return (t * cos_t + pltpu.roll(t, hd // 2, 1) * sin_t).astype(BF16)

    k_ref[...] = rope(dot(h, wk_ref[...]) + bk_ref[...].astype(F32))
    v_ref[...] = (dot(h, wv_ref[...]) + bv_ref[...].astype(F32)).astype(BF16)
    qf = dot(h, wq_ref[...]) + bq_ref[...].astype(F32)
    for n in range(nh):
        q_ref[n] = rope(qf[:, n * hd:(n + 1) * hd])


def qkv_proj(core, h, wq, wk, wv, bq, bk, bv, cos_t, sin_t, nh, hd, tm=256):
    rows, width = h.shape
    qw = nh * hd
    row = pl.BlockSpec((tm, hd), lambda i, c: (i, 0))
    grid_spec = pltpu.PrefetchScalarGridSpec(
        num_scalar_prefetch=1,
        grid=(rows // tm,),
        in_specs=[
            pl.BlockSpec((tm, width), lambda i, c: (i, 0)),
            pl.BlockSpec((width, qw), lambda i, c: (0, c[0])),
            pl.BlockSpec((width, hd), lambda i, c: (0, c[0])),
            pl.BlockSpec((width, hd), lambda i, c: (0, c[0])),
            pl.BlockSpec((1, qw), lambda i, c: (0, c[0])),
            pl.BlockSpec((1, hd), lambda i, c: (0, c[0])),
            pl.BlockSpec((1, hd), lambda i, c: (0, c[0])),
            row, row],
        out_specs=[pl.BlockSpec((nh, tm, hd), lambda i, c: (0, i, 0)), row, row])
    return pl.pallas_call(
        functools.partial(qkv_body, nh, hd),
        grid_spec=grid_spec,
        out_shape=[jax.ShapeDtypeStruct((nh, rows, hd), BF16),
                   jax.ShapeDtypeStruct((rows, hd), BF16), jax.ShapeDtypeStruct((rows, hd), BF16)],
        compiler_params=params(1),
        cost_estimate=pl.CostEstimate(flops=2 * rows * width * (qw + 2 * hd), bytes_accessed=8 << 20, transcendentals=0),
        name="qkv_proj",
    )(core, h, wq, wk, wv, bq, bk, bv, cos_t, sin_t)


def do_body(nh, hd, c_ref, d_ref, wo_ref, o_ref):
    r = dot_nt(d_ref[...], wo_ref[...]).astype(BF16)
    for n in range(nh):
        o_ref[n] = r[:, n * hd:(n + 1) * hd]


def do_proj(core, d, wo, nh, hd, tm=256):
    rows, width = d.shape
    qw = nh * hd
    grid_spec = pltpu.PrefetchScalarGridSpec(
        num_scalar_prefetch=1,
        grid=(rows // tm,),
        in_specs=[pl.BlockSpec((tm, width), lambda i, c: (i, 0)),
                  pl.BlockSpec((qw, width), lambda i, c: (c[0], 0))],
        out_specs=pl.BlockSpec((nh, tm, hd), lambda i, c: (0, i, 0)))
    return pl.pallas_call(
        functools.partial(do_body, nh, hd),
        grid_spec=grid_spec,
        out_shape=jax.ShapeDtypeStruct((nh, rows, hd), BF16),
        compiler_params=params(1),
        cost_estimate=pl.CostEstimate(flops=2 * rows * width * qw, bytes_accessed=6 << 20, transcendentals=0),
        name="do_proj",
    )(core, d, wo)


def attn_body(nh, hd, tile, pieces, scale, ids, own, q_ref, do_ref, k_ref, v_ref, cos_ref, sin_ref, dki_ref, dvi_ref,
              o_ref, dq_ref, dk_ref, dv_ref, ks, vs, kt, vt, ps, dps, ms, pb, dsb, ot, dqt):
    step = pl.program_id(0)
    tq = nh * tile
    c = scale * LOG2E

    @pl.when(step == 0)
    def _():
        for s in range(pieces):
            p = ids[s]
            kv = k_ref[s * tile:(s + 1) * tile, :]
            vv = v_ref[s * tile:(s + 1) * tile, :]
            ks[p] = kv
            vs[p] = vv
            kt[p] = kv.T
            vt[p] = vv.T
        dk_ref[...] = dki_ref[...]
        dv_ref[...] = dvi_ref[...]

    i = own[step]

    def first(j, carry, diag):
        m, l, dl = carry
        kj = ks[j]
        vj = vs[j]
        m_new, l_new, d_new = [], [], []
        for n in range(nh):
            lanes = slice(n * tile, (n + 1) * tile)
            s = dot_nt(kj, q_ref[n]) * c
            if diag:
                key = lax.broadcasted_iota(jnp.int32, (tile, tile), 0)
                qry = lax.broadcasted_iota(jnp.int32, (tile, tile), 1)
                s = jnp.where(key <= qry, s, NEG)
            dpb = dot_nt(vj, do_ref[n]).astype(BF16)
            dps[j, :, lanes] = dpb
            mo = m[:, lanes]
            mn = jnp.maximum(mo, jnp.max(s, axis=0, keepdims=True))
            p = jnp.exp2(s - mn)
            ps[j, :, lanes] = p
            al = jnp.exp2(mo - mn)
            m_new.append(mn)
            l_new.append(l[:, lanes] * al + jnp.sum(p, axis=0, keepdims=True))
            d_new.append(dl[:, lanes] * al + jnp.sum(p * dpb.astype(F32), axis=0, keepdims=True))
        m = jnp.concatenate(m_new, axis=1)
        ms[j] = m
        return m, jnp.concatenate(l_new, axis=1), jnp.concatenate(d_new, axis=1)

    init = (jnp.full((1, tq), NEG, F32), jnp.zeros((1, tq), F32), jnp.zeros((1, tq), F32))
    carry = lax.fori_loop(0, i, lambda j, cr: first(j, cr, False), init)
    m, l, dl = first(i, carry, True)
    inv = 1.0 / l
    delta = dl * inv
    ot[...] = jnp.zeros_like(ot)
    dqt[...] = jnp.zeros_like(dqt)

    def second(j, carry):
        f = jnp.exp2(ms[j] - m) * inv
        for n in range(nh):
            lanes = slice(n * tile, (n + 1) * tile)
            p = ps[j, :, lanes] * f[:, lanes]
            pb[:, lanes] = p.astype(BF16)
            dsb[:, lanes] = (p * (dps[j, :, lanes].astype(F32) - delta[:, lanes])).astype(BF16)
        ot[...] += dot(vt[j], pb[...])
        dqt[...] += dot(kt[j], dsb[...])
        dv_ref[j] += dot(pb[...], do_ref[...].reshape(tq, hd))
        dk_ref[j] += dot(dsb[...], q_ref[...].reshape(tq, hd))
        return carry

    lax.fori_loop(0, i + 1, second, 0)
    cos_t = cos_ref[...]
    sin_t = sin_ref[...]
    for n in range(nh):
        lanes = slice(n * tile, (n + 1) * tile)
        cols = slice(n * hd, (n + 1) * hd)
        o_ref[:, cols] = ot[:, lanes].T.astype(BF16)
        g = (dqt[:, lanes].T * scale).astype(BF16).astype(F32)
        dq_ref[:, cols] = (g * cos_t - pltpu.roll(g, hd // 2, 1) * sin_t).astype(BF16)


def attention(ids, own, q, do, k, v, cos_t, sin_t, dk, dv, scale, tile):
    nh, rows, hd = q.shape
    pieces = k.shape[0] // tile
    whole = k.shape[0]
    tq = nh * tile
    full2 = pl.BlockSpec((whole, hd), lambda i, a, b: (0, 0))
    acc = pl.BlockSpec((pieces, tile, hd), lambda i, a, b: (0, 0, 0))
    heads = pl.BlockSpec((nh, tile, hd), lambda i, a, b: (0, i, 0))
    table = pl.BlockSpec((tile, hd), lambda i, a, b: (i, 0))
    out = pl.BlockSpec((tile, nh * hd), lambda i, a, b: (i, 0))
    grid_spec = pltpu.PrefetchScalarGridSpec(
        num_scalar_prefetch=2,
        grid=(rows // tile,),
        in_specs=[heads, heads, full2, full2, table, table, acc, acc],
        out_specs=[out, out, acc, acc],
        scratch_shapes=[
            pltpu.VMEM((pieces, tile, hd), BF16), pltpu.VMEM((pieces, tile, hd), BF16),
            pltpu.VMEM((pieces, hd, tile), BF16), pltpu.VMEM((pieces, hd, tile), BF16),
            pltpu.VMEM((pieces, tile, tq), F32), pltpu.VMEM((pieces, tile, tq), BF16),
            pltpu.VMEM((pieces, 1, tq), F32),
            pltpu.VMEM((tile, tq), BF16), pltpu.VMEM((tile, tq), BF16),
            pltpu.VMEM((hd, tq), F32), pltpu.VMEM((hd, tq), F32)])
    return pl.pallas_call(
        functools.partial(attn_body, nh, hd, tile, pieces, scale),
        grid_spec=grid_spec,
        out_shape=[jax.ShapeDtypeStruct((rows, nh * hd), BF16), jax.ShapeDtypeStruct((rows, nh * hd), BF16),
                   jax.ShapeDtypeStruct((pieces, tile, hd), F32), jax.ShapeDtypeStruct((pieces, tile, hd), F32)],
        compiler_params=params(1),
        cost_estimate=pl.CostEstimate(flops=rows * whole * nh * hd * 12, bytes_accessed=8 << 20,
                                      transcendentals=rows * whole * nh),
        name="attn_fwd_bwd",
    )(ids, own, q, do, k, v, cos_t, sin_t, dk, dv)


def solution(mesh):
    groups = mesh.shape['cp']
    row_spec = P('dp', 'cp', None)
    mat_spec = P(('dp', 'cp'), None)
    vec_spec = P('dp')
    near = [(i, i ^ 1) for i in range(groups)]
    far = [(i, i ^ 2) for i in range(groups)]

    def swap(v):
        return lax.ppermute(v, 'cp', near)

    def cross(v):
        return lax.ppermute(v, 'cp', far)

    def device_fn(x_in, ln_w, ln_b, w_q, b_q, w_k, b_k, w_v, b_v, w_o, b_o, long_factor, dy_out):
        rank = lax.axis_index('cp')
        core = rank % 2
        chip = rank // 2
        x_rows = x_in[0]
        d0 = dy_out[0]
        tokens, width = x_rows.shape
        piece = tokens // 2
        hd = 2 * long_factor.shape[0]
        kv_heads = w_k.shape[1] // hd
        nh = w_q.shape[1] // hd // kv_heads
        qw = nh * hd
        scale = hd ** -0.5
        core_v = jnp.reshape(core, (1,)).astype(jnp.int32)

        h0 = layer_norm(x_rows, ln_w[None], ln_b[None])
        h2 = cross(h0)
        d2 = cross(d0)
        h1 = swap(h0)
        d1 = swap(d0)
        h3 = swap(h2)
        d3 = swap(d2)

        blocks = jnp.stack([rank, rank ^ 1, rank ^ 2, rank ^ 3]).astype(jnp.int32)
        ids = jnp.stack([blocks, 2 * groups - 1 - blocks], axis=1).reshape(2 * groups)
        pos = (ids[:, None] * piece + jnp.arange(piece, dtype=jnp.int32)[None, :]).reshape(2 * groups * piece)
        cos_t, sin_t = rope_tables(pos, long_factor)
        half = 2 * tokens

        def project(h, t):
            return qkv_proj(core_v, h, w_q, w_k, w_v, b_q[None], b_k[None], b_v[None], cos_t[t], sin_t[t], nh, hd)

        lo = slice(0, half)
        hi = slice(half, 2 * half)
        h01 = jnp.concatenate([h0, h1], axis=0)
        d01 = jnp.concatenate([d0, d1], axis=0)
        h23 = jnp.concatenate([h2, h3], axis=0)
        d23 = jnp.concatenate([d2, d3], axis=0)
        q01, k01, v01 = project(h01, lo)
        do01 = do_proj(core_v, d01, w_o, nh, hd)
        q23, k23, v23 = project(h23, hi)
        k_all = jnp.concatenate([k01, k23], axis=0)
        v_all = jnp.concatenate([v01, v23], axis=0)
        zero = jnp.zeros((2 * groups, piece, hd), F32)
        o01, dq01, dk_a, dv_a = attention(ids, ids[:4], q01, do01, k_all, v_all, cos_t[lo], sin_t[lo], zero, zero, scale, piece)
        do23 = do_proj(core_v, d23, w_o, nh, hd)
        o23, dq23, dk_s, dv_s = attention(ids, ids[4:], q23, do23, k_all, v_all, cos_t[hi], sin_t[hi], dk_a, dv_a, scale, piece)

        both = jnp.stack([o01[tokens:], dq01[tokens:]])
        other = swap(both)
        first = core == 0

        def by_head(mine, theirs):
            return jnp.where(first, jnp.concatenate([mine, theirs], axis=1), jnp.concatenate([theirs, mine], axis=1))

        attn_rows = by_head(o01[:tokens], other[0])
        dq_rows = by_head(dq01[:tokens], other[1])
        y_rows = (x_rows.astype(F32) + dot(attn_rows, w_o) + b_o.astype(F32)).astype(BF16)

        dk_r = jnp.take(dk_s, ids, axis=0).reshape(2 * half, hd) * scale
        dv_r = jnp.take(dv_s, ids, axis=0).reshape(2 * half, hd)
        dk_r = dk_r.astype(BF16).astype(F32)
        dk_b = (dk_r * cos_t - jnp.roll(dk_r, hd // 2, axis=1) * sin_t).astype(BF16)
        dv_b = dv_r.astype(BF16)
        dkv_b = jnp.concatenate([dk_b, dv_b], axis=1)
        dkv_o = swap(dkv_b[tokens:half])
        dkv_m = dkv_b[:tokens]
        dk_rows = by_head(dkv_m[:, :hd], dkv_o[:, :hd])
        dv_rows = by_head(dkv_m[:, hd:], dkv_o[:, hd:])

        d_hid = (dot_nt(dq_rows, w_q) + dot_nt(dk_rows, w_k) + dot_nt(dv_rows, w_v)).astype(BF16).astype(F32)
        x_f = x_rows.astype(F32)
        cen = x_f - jnp.mean(x_f, axis=-1, keepdims=True)
        inv_std = lax.rsqrt(jnp.mean(cen * cen, axis=-1, keepdims=True) + EPS)
        x_hat = cen * inv_std
        a6 = d_hid * ln_w.astype(F32)
        d_x = inv_std * (a6 - jnp.mean(a6, axis=-1, keepdims=True) - x_hat * jnp.mean(a6 * x_hat, axis=-1, keepdims=True))
        dx_rows = (d0.astype(F32) + d_x).astype(BF16)

        h_cols = jnp.concatenate([lax.dynamic_slice(h, (0, chip * (width // 2)), (half, width // 2)) for h in (h01, h23)], axis=0)
        dqkv = jnp.concatenate([jnp.concatenate([dq01, dq23], axis=0), dkv_b], axis=1)
        d_w = dot_tn(h_cols, dqkv)
        part = width // groups
        mine = lax.dynamic_slice(d_w, (core * part, 0), (part, qw + 2 * hd))
        theirs = swap(lax.dynamic_slice(d_w, ((1 - core) * part, 0), (part, qw + 2 * hd)))
        d_wq = by_head(mine[:, :qw], theirs[:, :qw])
        d_wk = by_head(mine[:, qw:qw + hd], theirs[:, qw:qw + hd])
        d_wv = by_head(mine[:, qw + hd:], theirs[:, qw + hd:])

        o_all = jnp.concatenate([o01, o23], axis=0)
        o_mine = lax.dynamic_slice(o_all, (0, core * part), (2 * half, part))
        o_send = lax.dynamic_slice(o_all, (0, (1 - core) * part), (2 * half, part)).reshape(2, 2, tokens, part)
        o_got = swap(o_send[:, ::-1].reshape(2 * half, part))
        o_cols = jnp.where(core == chip, o_mine, o_got)
        d_wo = dot_tn(o_cols, jnp.concatenate([d01, d23], axis=0))

        sums = jnp.concatenate([jnp.sum(dq01.astype(F32), axis=0), jnp.sum(dkv_b[:half].astype(F32), axis=0)])
        gap = jnp.zeros_like(sums)
        sums = jnp.where(first, jnp.stack([sums, gap]), jnp.stack([gap, sums])).reshape(-1)
        vec = jnp.concatenate([jnp.sum(d_hid * x_hat, axis=0), jnp.sum(d_hid, axis=0), jnp.sum(d0.astype(F32), axis=0), sums])
        vec = vec + swap(vec)
        vec = vec + cross(vec)
        d_lnw = vec[:width]
        d_lnb = vec[width:2 * width]
        d_bo = vec[2 * width:3 * width]
        per = vec[3 * width:].reshape(kv_heads, qw + 2 * hd)
        d_bq = per[:, :qw].reshape(-1)
        d_bk = per[:, qw:qw + hd].reshape(-1)
        d_bv = per[:, qw + hd:].reshape(-1)
        return (y_rows[None], dx_rows[None], d_wq, d_wk, d_wv, d_wo, d_lnw, d_lnb, d_bq, d_bk, d_bv, d_bo)

    in_specs = (row_spec,) + (P(),) * 11 + (row_spec,)
    out_specs = (row_spec, row_spec) + (mat_spec,) * 4 + (vec_spec,) * 6
    return jax.shard_map(device_fn, mesh=mesh, in_specs=in_specs, out_specs=out_specs, check_vma=False)
```

time: 433 us -> 253 us (0.58)
  matrix products: 223 us -> 20.7 us
  Pallas kernels: 0 us -> 104 us
  waiting for transfers between devices: 137 us -> 55.3 us
  local copies, waits for them, and re-layouts: 15.3 us -> 30.2 us
  between operations: 15 us -> 1.46 us
  blocking collectives: 12.9 us -> 0 us
  other arithmetic: 25.1 us -> 32.3 us
  starting transfers between devices: 1.24 us -> 7.28 us
    dot_general x17 -> x6, matrix products: 196 us -> 20.7 us  [the longest x2 11.5 us: dot_tn(): lax.dot_general(a, b, (((0,), (0,)), ((), ())), preferred_element_type=F32)]
    reduce_scatter x5 -> x0, waiting for transfers between devices: 136 us -> none  [the longest x4 96.5 us: device_fn(): lax.psum_scatter(grad_mat, 'cp', scatter_dimension=0, tiled=True)]
    pallas_call x0 -> x7, Pallas kernels: none -> 104 us  [the longest x2 78.9 us: attention(): pl.pallas_call(functools.partial(attn_body, nh, hd, tile, pieces, scale),...]
    ppermute x0 -> x12, waiting for transfers between devices: none -> 55.3 us  [the longest x3 55.3 us: cross(): return lax.ppermute(v, 'cp', far)]
    sub x1 -> x0, matrix products: 26.7 us -> none  [device_fn(): probs = jax.nn.softmax(jnp.where(visible, scores, -1e+30), axis=-1)]
    psum x1 -> x0, blocking collectives: 12.9 us -> none  [device_fn(): d_vecs = lax.psum((d_lnw, d_lnb, d_bq, d_bk, d_bv, d_bo), 'cp')]
    concatenate x2 -> x7, other arithmetic: 0.15 us -> 12.3 us  [the longest x2 6.23 us: device_fn(): h01 = jnp.concatenate([h0, h1], axis=0)]
    unnamed x69 -> x104, local copies, waits for them, and re-layouts: 6.21 us -> 13.8 us
  transfers between devices with their start and end apart: 6 -> 12, of which waited for: 3 -> 3; matrix products, arithmetic and copies ran while one was open for 30% -> 23% of each run, Pallas kernels for 0% -> 23%
where the time goes in v1:
time: 253 us; the launch traced here: 252 us
  Pallas kernels  104 us (41%)
  waiting for transfers between devices  55.3 us (22%)
  other arithmetic  32.3 us (13%)
  local copies, waits for them, and re-layouts  30.2 us (12%)
  matrix products  20.7 us (8%)
  starting transfers between devices  7.28 us (3%)
    pallas_call x2, Pallas kernels, attention(): pl.pallas_call(functools.partial(attn_body, nh, hd, tile, pieces, scale),...  78.9 us
    ppermute x3, waiting for transfers between devices, cross(): return lax.ppermute(v, 'cp', far)  55.3 us
    pallas_call x2, Pallas kernels, qkv_proj(): pl.pallas_call(functools.partial(qkv_body, nh, hd), grid_spec=grid_spec,...  14.4 us
    unnamed x104, local copies, waits for them, and re-layouts  13.8 us
    dot_general x2, matrix products, dot_tn(): lax.dot_general(a, b, (((0,), (0,)), ((), ())), preferred_element_type=F32)  11.5 us
    pallas_call x2, Pallas kernels, do_proj(): pl.pallas_call(functools.partial(do_body, nh, hd), grid_spec=grid_spec, o...  10 us
    concatenate x2, other arithmetic, device_fn(): h01 = jnp.concatenate([h0, h1], axis=0)  6.23 us
    dot_general x3, matrix products, dot_nt(): lax.dot_general(a, b, (((1,), (1,)), ((), ())), preferred_element_type=F32)  5.19 us
  transfers between devices with their start and end apart: 12, of which 3 were waited for; matrix products, arithmetic and copies ran while one was open for 23% of the time, Pallas kernels for 23%

profile of v1, /device:TPU:0, one launch (start us, length us, event | category | flops | bytes accessed | tf_op | source)
XLA Modules:
  0.0 251.7 jit_solution(13893333851604799855)
XLA Ops:
  4.6 3.3 %collective-permute-start.2 = (bf16[512,1536]{1,0:T(8,128)(2,1)S(1)}, bf16[512,1536]{1,0:T(8,128)(2,1)}, u32[]{:S(2)}, u32[]{:S(2)}) collective-permute-start(bf16[512,1536]{1,0:T(8,128)(2,1)S(1)} %ln_rows.1), channel_id=1, source_target_pairs={{0,2},{1,3},{2,0},{3,1},{4,6},{5,7},{6,4},{7,5},{8,10},{9,11},{10,... | collective-permute-start | bytes 4718600 | tf_op jit(solution)/shard_map/ppermute | solution.py:261
  8.9 3.8 %fusion.54 = (f32[2048,64]{1,0:T(8,128)S(1)}, f32[2048,64]{1,0:T(8,128)S(1)}, f32[2048,64]{1,0:T(8,128)S(1)}) fusion(f32[64]{0:T(128)S(1)} %multiply_divide_fusion, f32[2048]{0:T(1024)S(1)} %bitcast.70), kind=kLoop, calls=%fused_computation.78 | loop fusion | flops 524288 | bytes 1581312 | tf_op jit(solution)/shard_map/mul | solution.py:37
  14.3 1.9 fusion.59
  18.7 24.4 %collective-permute-done.2 = bf16[512,1536]{1,0:T(8,128)(2,1)} collective-permute-done((bf16[512,1536]{1,0:T(8,128)(2,1)S(1)}, bf16[512,1536]{1,0:T(8,128)(2,1)}, u32[]{:S(2)}, u32[]{:S(2)}) %collective-permute-start.2) | collective-permute-done | bytes 1572896 | tf_op jit(solution)/shard_map/ppermute | solution.py:261
  43.1 3.2 %pad_maximum_fusion.h_ref = bf16[1024,1536]{1,0:T(8,128)(2,1)} fusion(bf16[512,1536]{1,0:T(8,128)(2,1)} %collective-permute-done, bf16[512,1536]{1,0:T(8,128)(2,1)S(1)} %ln_rows.1), kind=kLoop, calls=%fused_computation.33 | loop fusion | flops 6291456 | bytes 6291456 | tf_op jit(solution)/shard_map/concatenate | solution.py:297
  46.4 29.6 %collective-permute-done.5 = bf16[512,1536]{1,0:T(8,128)(2,1)} collective-permute-done((bf16[512,1536]{1,0:T(8,128)(2,1)}, bf16[512,1536]{1,0:T(8,128)(2,1)}, u32[]{:S(2)}, u32[]{:S(2)}) %collective-permute-start.5) | collective-permute-done | bytes 1572896 | tf_op jit(solution)/shard_map/ppermute | solution.py:261
  76.0 7.2 %qkv_proj.2 = (bf16[6,1024,128]{2,1,0:T(8,128)(2,1)S(1)}, bf16[1024,128]{1,0:T(8,128)(2,1)S(1)}, bf16[1024,128]{1,0:T(8,128)(2,1)S(1)}) custom-call(s32[1]{0:T(128)} %bitcast.10.c_ref, bf16[1024,1536]{1,0:T(8,128)(2,1)} %pad_maximum_fusion.h_ref, bf16[1536,1536]{1,0:T(8,128)(2,1)} %wq_ref.3, bf16[1536,256]{1,0:T(8,128)(2,1)S(1)} %copy-done.4, ...), custom_call_target="tpu_custom_call" | custom-call | flops 3221225472 | bytes 8388608 | tf_op jit(solution)/shard_map/qkv_proj/pallas_call | solution.py:100
  83.3 3.0 %fusion.36 = bf16[1024,768]{1,0:T(8,128)(2,1)} fusion(s32[]{:T(128)S(6)} %select_n.99, bf16[512,1536]{1,0:T(8,128)(2,1)S(1)} %ln_rows.1, bf16[512,1536]{1,0:T(8,128)(2,1)} %collective-permute-done), kind=kLoop, calls=%fused_computation.55 | loop fusion | flops 3145728 | bytes 4718596 | tf_op jit(solution)/shard_map/concatenate | solution.py:297
  86.3 2.1 pad_maximum_fusion.1.d_ref
  88.4 5.0 %do_proj.2.do_ref = bf16[6,1024,128]{2,1,0:T(8,128)(2,1)S(1)} custom-call(s32[1]{0:T(128)} %bitcast.10.c_ref, bf16[1024,1536]{1,0:T(8,128)(2,1)S(1)} %pad_maximum_fusion.1.d_ref, bf16[1536,1536]{1,0:T(8,128)(2,1)} %wo_ref.3), custom_call_target="tpu_custom_call" | custom-call | flops 2415919104 | bytes 6291456 | tf_op jit(solution)/shard_map/do_proj/pallas_call | solution.py:126
  93.5 2.1 constant_dynamic-update-slice_fusion.1
  95.6 1.5 constant_dynamic-update-slice_fusion.h_ref
  97.1 1.6 copy-done.30
  98.7 7.2 %qkv_proj.3 = (bf16[6,1024,128]{2,1,0:T(8,128)(2,1)S(1)}, bf16[1024,128]{1,0:T(8,128)(2,1)S(1)}, bf16[1024,128]{1,0:T(8,128)(2,1)S(1)}) custom-call(s32[1]{0:T(128)} %bitcast.10.c_ref, bf16[1024,1536]{1,0:T(8,128)(2,1)} %copy-done.30, bf16[1536,1536]{1,0:T(8,128)(2,1)} %wq_ref.3, bf16[1536,256]{1,0:T(8,128)(2,1)S(1)} %copy-done.4, ...), custom_call_target="tpu_custom_call" | custom-call | flops 3221225472 | bytes 8388608 | tf_op jit(solution)/shard_map/qkv_proj/pallas_call | solution.py:100
  106.1 39.3 %attn_fwd_bwd.2 = (bf16[1024,768]{1,0:T(8,128)(2,1)}, bf16[1024,768]{1,0:T(8,128)(2,1)}, f32[8,256,128]{2,1,0:T(8,128)S(1)}, f32[8,256,128]{2,1,0:T(8,128)S(1)}) custom-call(s32[8]{0:T(128)S(1)} %reshape.171.ids, s32[4]{0:T(128)S(1)} %slice.120.own, bf16[6,1024,128]{2,1,0:T(8,128)(2,1)} %copy-done.13, bf16[6,1024,128]{2,1,0:T(8,128)(2,1)} %copy-done.2, ...), custom_call_target="tpu_custom_call" | custom-call | flops 19327352832 | bytes 8388608 | tf_op jit(solution)/shard_map/attn_fwd_bwd/pallas_call | solution.py:237
  145.4 2.1 convert_reduce_fusion.3
  147.5 2.6 %fusion.84 = (bf16[512,768]{1,0:T(8,128)(2,1)}, bf16[1,512,768]{2,1,0:T(8,128)(2,1)}) fusion(bf16[1024,768]{1,0:T(8,128)(2,1)} %get-tuple-element.33), kind=kLoop, calls=%fused_computation.163 | loop fusion | bytes 3145728 | tf_op jit(solution)/shard_map/slice | solution.py:319
  150.1 2.1 pad_maximum_fusion.2.d_ref
  152.2 5.0 %do_proj.3.do_ref = bf16[6,1024,128]{2,1,0:T(8,128)(2,1)S(1)} custom-call(s32[1]{0:T(128)} %bitcast.10.c_ref, bf16[1024,1536]{1,0:T(8,128)(2,1)S(1)} %pad_maximum_fusion.2.d_ref, bf16[1536,1536]{1,0:T(8,128)(2,1)} %wo_ref.3), custom_call_target="tpu_custom_call" | custom-call | flops 2415919104 | bytes 6291456 | tf_op jit(solution)/shard_map/do_proj/pallas_call | solution.py:126
  158.4 39.6 %attn_fwd_bwd.3 = (bf16[1024,768]{1,0:T(8,128)(2,1)}, bf16[1024,768]{1,0:T(8,128)(2,1)}, f32[8,256,128]{2,1,0:T(8,128)S(1)}, f32[8,256,128]{2,1,0:T(8,128)S(1)}) custom-call(s32[8]{0:T(128)S(1)} %reshape.171.ids, s32[4]{0:T(128)S(1)} %slice.132.own, bf16[6,1024,128]{2,1,0:T(8,128)(2,1)} %copy-done.14, bf16[6,1024,128]{2,1,0:T(8,128)(2,1)} %copy-done.3, ...), custom_call_target="tpu_custom_call" | custom-call | flops 19327352832 | bytes 8388608 | tf_op jit(solution)/shard_map/attn_fwd_bwd/pallas_call | solution.py:237
  198.9 1.6 gather_fusion
  200.5 1.9 gather_fusion.1
  209.5 1.7 copy-done.28
  213.2 1.8 pad_maximum_fusion.3
  215.8 5.6 %fusion.11 = f32[768,1024]{1,0:T(8,128)S(1)} fusion(bf16[2048,128]{1,0:T(8,128)(2,1)S(1)} %bitcast.65, bf16[2048,128]{1,0:T(8,128)(2,1)S(1)} %copy-done.25, bf16[1024,768]{1,0:T(8,128)(2,1)} %get-tuple-element.39, bf16[1024,768]{1,0:T(8,128)(2,1)S(1)} %copy-done.22, bf16[1024,768]{1,0:T(8,128)(2,1)S(1)} %constant_dynamic-slice_fusion.3, ...), kind=kOutput, calls=%fused_computation.19 | convolution fusion | flops 3244294144 | bytes 10485760 | tf_op jit(solution)/shard_map/dot_general | solution.py:28
  223.6 2.6 %fusion.42 = f32[512,1536]{1,0:T(8,128)S(1)} fusion(bf16[1536,1536]{1,0:T(8,128)(2,1)S(1)} %bitcast.73, bf16[512,768]{1,0:T(8,128)(2,1)S(1)} %get-tuple-element.55, bf16[512,768]{1,0:T(8,128)(2,1)S(1)} %copy-done.33, pred[]{:T(512)S(6)} %eq.8), kind=kOutput, calls=%fused_computation.64 | convolution fusion | flops 2422996992 | bytes 9437185 | tf_op jit(solution)/shard_map/dot_general | solution.py:24
  227.4 1.9 fusion.28
  229.4 4.0 %convert_reduce_fusion.2 = (f32[1536]{0:T(1024)S(1)}, bf16[1,512,1536]{2,1,0:T(8,128)(2,1)}) fusion(bf16[1,512,1536]{2,1,0:T(8,128)(2,1)} %param.27, f32[512]{0:T(512)S(1)} %broadcast_multiply_fusion, f32[512]{0:T(512)S(1)} %copy-done.36, bf16[1,512,1536]{2,1,0:T(8,128)(2,1)S(1)} %copy-done.1, f32[512]{0:T(512)S(1)} %broadcast_multiply_fusion.1, ...), kind=kLoop, calls=%fused_computation.27 | loop fusion | flops 10222080 | bytes 6311936 | tf_op jit(solution)/shard_map/reduce_sum | solution.py:362
  233.6 1.7 maximum_select_fusion
  235.3 4.0 %fusion.34 = bf16[1,512,1536]{2,1,0:T(8,128)(2,1)} fusion(bf16[1536,1536]{1,0:T(8,128)(2,1)S(1)} %bitcast.61, bf16[512,768]{1,0:T(8,128)(2,1)S(1)} %get-tuple-element.56, bf16[512,768]{1,0:T(8,128)(2,1)S(1)} %copy-done.34, f32[1536]{0:T(1024)S(1)} %copy-done.39, pred[]{:T(512)S(6)} %eq.8, bf16[1,512,1536]{2,1,0:T(8,128)(2,1)S(1)} %copy-done.1), kind=kOutput, calls=%fused_computation.52 | convolution fusion | flops 2426142720 | bytes 9443329 | tf_op jit(solution)/shard_map/dot_general | solution.py:20
  239.3 5.9 %fusion = f32[384,1536]{1,0:T(8,128)} fusion(bf16[512,1536]{1,0:T(8,128)(2,1)} %collective-permute-done.6, bf16[512,1536]{1,0:T(8,128)(2,1)} %collective-permute-done.5, bf16[512,1536]{1,0:T(8,128)(2,1)} %collective-permute-done.1, bf16[512,1536]{1,0:T(8,128)(2,1)} %bitcast.11, bf16[2048,384]{1,0:T(8,128)(2,1)S(1)} %collective-permute-done.9, ...), kind=kOutput, calls=%fused_computation.2 | convolution fusion | flops 2441871360 | bytes 11796485 | tf_op jit(solution)/shard_map/dot_general | solution.py:28
  246.0 1.8 collective-permute-start.11
  (191 shorter events, 29.3 us)
Async XLA Ops:
  0.6 7.8 %copy-start.42 = (f32[64]{0:T(128)S(1)}, f32[64]{0:T(128)}, u32[]{:S(2)}) copy-start(f32[64]{0:T(128)} %param.26) | copy-start | bytes 772
  4.6 38.5 %collective-permute-start.2 = (bf16[512,1536]{1,0:T(8,128)(2,1)S(1)}, bf16[512,1536]{1,0:T(8,128)(2,1)}, u32[]{:S(2)}, u32[]{:S(2)}) collective-permute-start(bf16[512,1536]{1,0:T(8,128)(2,1)S(1)} %ln_rows.1), channel_id=1, source_target_pairs={{0,2},{1,3},{2,0},{3,1},{4,6},{5,7},{6,4},{7,5},{8,10},{9,11},{10,... | collective-permute-start | bytes 4718600 | tf_op jit(solution)/shard_map/ppermute | solution.py:261
  7.9 35.3 %collective-permute-start = (bf16[512,1536]{1,0:T(8,128)(2,1)S(1)}, bf16[512,1536]{1,0:T(8,128)(2,1)}, u32[]{:S(2)}, u32[]{:S(2)}) collective-permute-start(bf16[512,1536]{1,0:T(8,128)(2,1)S(1)} %ln_rows.1), channel_id=1, source_target_pairs={{0,1},{1,0},{2,3},{3,2},{4,5},{5,4},{6,7},{7,6},{8,9},{9,8},{10,11... | collective-permute-start | bytes 4718600 | tf_op jit(solution)/shard_map/ppermute | solution.py:258
  7.9 68.1 %collective-permute-start.5 = (bf16[512,1536]{1,0:T(8,128)(2,1)}, bf16[512,1536]{1,0:T(8,128)(2,1)}, u32[]{:S(2)}, u32[]{:S(2)}) collective-permute-start(bf16[512,1536]{1,0:T(8,128)(2,1)} %bitcast.11), channel_id=1, source_target_pairs={{0,2},{1,3},{2,0},{3,1},{4,6},{5,7},{6,4},{7,5},{8,10},{9,11},{10,... | collective-permute-start | bytes 4718600 | tf_op jit(solution)/shard_map/ppermute | solution.py:261
  8.0 78.3 %collective-permute-start.1 = (bf16[512,1536]{1,0:T(8,128)(2,1)}, bf16[512,1536]{1,0:T(8,128)(2,1)}, u32[]{:S(2)}, u32[]{:S(2)}) collective-permute-start(bf16[512,1536]{1,0:T(8,128)(2,1)} %bitcast.11), channel_id=1, source_target_pairs={{0,1},{1,0},{2,3},{3,2},{4,5},{5,4},{6,7},{7,6},{8,9},{9,8},{10,11... | collective-permute-start | bytes 4718600 | tf_op jit(solution)/shard_map/ppermute | solution.py:258
  12.7 3.5 %copy-start.37 = (bf16[1536]{0:T(1024)(128)(2,1)S(1)}, bf16[1536]{0:T(1024)(128)(2,1)}, u32[]{:S(2)}) copy-start(bf16[1536]{0:T(1024)(128)(2,1)} %param.16) | copy-start | bytes 9220
  12.7 3.5 %copy-start.44 = (bf16[256]{0:T(256)(128)(2,1)S(1)}, bf16[256]{0:T(256)(128)(2,1)}, u32[]{:S(2)}) copy-start(bf16[256]{0:T(256)(128)(2,1)} %param.23) | copy-start | bytes 1540
  12.7 3.9 %copy-start.41 = (bf16[1536]{0:T(1024)(128)(2,1)S(1)}, bf16[1536]{0:T(1024)(128)(2,1)}, u32[]{:S(2)}) copy-start(bf16[1536]{0:T(1024)(128)(2,1)} %param.19) | copy-start | bytes 9220
  12.7 3.9 %copy-start.40 = (bf16[1536]{0:T(1024)(128)(2,1)S(1)}, bf16[1536]{0:T(1024)(128)(2,1)}, u32[]{:S(2)}) copy-start(bf16[1536]{0:T(1024)(128)(2,1)} %param.25) | copy-start | bytes 9220
  12.7 4.5 %copy-start.1 = (bf16[1,512,1536]{2,1,0:T(8,128)(2,1)S(1)}, bf16[1,512,1536]{2,1,0:T(8,128)(2,1)}, u32[]{:S(2)}) copy-start(bf16[1,512,1536]{2,1,0:T(8,128)(2,1)} %param.15) | copy-start | bytes 4718596
  17.6 28.8 %copy-start.35 = (f32[512]{0:T(512)}, f32[512]{0:T(512)S(1)}, u32[]{:S(2)}) copy-start(f32[512]{0:T(512)S(1)} %broadcast_multiply_fusion.2) | copy-start | bytes 6148
  18.7 57.3 %copy-start.4 = (bf16[1536,256]{1,0:T(8,128)(2,1)S(1)}, bf16[1536,256]{1,0:T(8,128)(2,1)}, u32[]{:S(2)}) copy-start(bf16[1536,256]{1,0:T(8,128)(2,1)} %wk_ref.3) | copy-start | bytes 2359300
  18.7 57.3 %copy-start.8 = (f32[1024,128]{1,0:T(8,128)S(1)}, f32[1024,128]{1,0:T(8,128)}, u32[]{:S(2)}) copy-start(f32[1024,128]{1,0:T(8,128)} %get-tuple-element.48.sin_ref) | copy-start | bytes 1572868
  18.7 57.3 %copy-start.9 = (f32[1024,128]{1,0:T(8,128)S(1)}, f32[1024,128]{1,0:T(8,128)}, u32[]{:S(2)}) copy-start(f32[1024,128]{1,0:T(8,128)} %get-tuple-element.78.cos_ref) | copy-start | bytes 1572868
  18.7 57.3 %copy-start.11 = (bf16[1536,256]{1,0:T(8,128)(2,1)S(1)}, bf16[1536,256]{1,0:T(8,128)(2,1)}, u32[]{:S(2)}) copy-start(bf16[1536,256]{1,0:T(8,128)(2,1)} %wv_ref.3) | copy-start | bytes 2359300
  43.1 52.4 %collective-permute-start.3 = (bf16[512,1536]{1,0:T(8,128)(2,1)}, bf16[512,1536]{1,0:T(8,128)(2,1)}, u32[]{:S(2)}, u32[]{:S(2)}) collective-permute-start(bf16[512,1536]{1,0:T(8,128)(2,1)} %collective-permute-done.2), channel_id=1, source_target_pairs={{0,1},{1,0},{2,3},{3,2},{4,5},{5,4},{6,7},{7,6},{8,9},{9,8},{10,11... | collective-permute-start | bytes 4718600 | tf_op jit(solution)/shard_map/ppermute | solution.py:258
  76.0 74.1 %collective-permute-start.6 = (bf16[512,1536]{1,0:T(8,128)(2,1)}, bf16[512,1536]{1,0:T(8,128)(2,1)}, u32[]{:S(2)}, u32[]{:S(2)}) collective-permute-start(bf16[512,1536]{1,0:T(8,128)(2,1)} %collective-permute-done.5), channel_id=1, source_target_pairs={{0,1},{1,0},{2,3},{3,2},{4,5},{5,4},{6,7},{7,6},{8,9},{9,8},{10,11... | collective-permute-start | bytes 4718600 | tf_op jit(solution)/shard_map/ppermute | solution.py:258
  93.4 3.7 %copy-start.2 = (bf16[6,1024,128]{2,1,0:T(8,128)(2,1)}, bf16[6,1024,128]{2,1,0:T(8,128)(2,1)S(1)}, u32[]{:S(2)}) copy-start(bf16[6,1024,128]{2,1,0:T(8,128)(2,1)S(1)} %do_proj.2.do_ref) | copy-start | bytes 4718596
  93.4 5.3 %copy-start.6 = (f32[1024,128]{1,0:T(8,128)S(1)}, f32[1024,128]{1,0:T(8,128)}, u32[]{:S(2)}) copy-start(f32[1024,128]{1,0:T(8,128)} %get-tuple-element.47.sin_ref) | copy-start | bytes 1572868
  93.4 5.3 %copy-start.7 = (f32[1024,128]{1,0:T(8,128)S(1)}, f32[1024,128]{1,0:T(8,128)}, u32[]{:S(2)}) copy-start(f32[1024,128]{1,0:T(8,128)} %get-tuple-element.79.cos_ref) | copy-start | bytes 1572868
  105.9 39.5 %copy-start.14 = (bf16[6,1024,128]{2,1,0:T(8,128)(2,1)}, bf16[6,1024,128]{2,1,0:T(8,128)(2,1)S(1)}, u32[]{:S(2)}) copy-start(bf16[6,1024,128]{2,1,0:T(8,128)(2,1)S(1)} %get-tuple-element.34.q_ref) | copy-start | bytes 4718596
  145.4 4.7 %copy-start.15 = (f32[8,256,128]{2,1,0:T(8,128)}, f32[8,256,128]{2,1,0:T(8,128)S(1)}, u32[]{:S(2)}) copy-start(f32[8,256,128]{2,1,0:T(8,128)S(1)} %get-tuple-element.36.dvi_ref) | copy-start | bytes 3145732
  208.8 13.5 %collective-permute-start.7 = (bf16[512,256]{1,0:T(8,128)(2,1)S(1)}, bf16[512,256]{1,0:T(8,128)(2,1)}, u32[]{:S(2)}, u32[]{:S(2)}) collective-permute-start(bf16[512,256]{1,0:T(8,128)(2,1)S(1)} %pad_maximum_fusion.5), channel_id=1, source_target_pairs={{0,1},{1,0},{2,3},{3,2},{4,5},{5,4},{6,7},{7,6},{8,9},{9,8},{10,11... | collective-permute-start | bytes 786440 | tf_op jit(solution)/shard_map/ppermute | solution.py:258
  212.6 26.7 %collective-permute-start.9 = (bf16[2048,384]{1,0:T(8,128)(2,1)}, bf16[2048,384]{1,0:T(8,128)(2,1)S(1)}, u32[]{:S(2)}, u32[]{:S(2)}) collective-permute-start(bf16[2048,384]{1,0:T(8,128)(2,1)} %bitcast.66), channel_id=1, source_target_pairs={{0,1},{1,0},{2,3},{3,2},{4,5},{5,4},{6,7},{7,6},{8,9},{9,8},{10,11... | collective-permute-start | bytes 4718600 | tf_op jit(solution)/shard_map/ppermute | solution.py:258
  213.2 10.4 %slice-start.3 = ((s8[4718592]{0:T(1024)(128)(4,1)}), s8[4194304]{0:T(1024)(128)(4,1)S(1)}, s32[]{:S(2)}) async-start(s8[4718592]{0:T(1024)(128)(4,1)} %bitcast.72), calls=%async_computation.3 | async-start | bytes 8388608
  214.9 8.5 %collective-permute-start.4 = (bf16[2,512,768]{2,1,0:T(8,128)(2,1)S(1)}, bf16[2,512,768]{2,1,0:T(8,128)(2,1)S(1)}, u32[]{:S(2)}, u32[]{:S(2)}) collective-permute-start(bf16[2,512,768]{2,1,0:T(8,128)(2,1)S(1)} %pad_maximum_fusion.3), channel_id=1, source_target_pairs={{0,1},{1,0},{2,3},{3,2},{4,5},{5,4},{6,7},{7,6},{8,9},{9,8},{10,11... | collective-permute-start | bytes 4718600 | tf_op jit(solution)/shard_map/ppermute | solution.py:258
  215.8 7.7 %slice-start.4 = ((s8[4718592]{0:T(1024)(128)(4,1)}), s8[524288]{0:T(1024)(128)(4,1)S(1)}, s32[]{:S(2)}) async-start(s8[4718592]{0:T(1024)(128)(4,1)} %bitcast.72), calls=%async_computation.4 | async-start | bytes 1048576
  221.6 11.8 %collective-permute-start.8 = (f32[384,1024]{1,0:T(8,128)S(1)}, f32[384,1024]{1,0:T(8,128)S(1)}, u32[]{:S(2)}, u32[]{:S(2)}) collective-permute-start(f32[384,1024]{1,0:T(8,128)S(1)} %constant_dynamic-slice_fusion.2), channel_id=1, source_target_pairs={{0,1},{1,0},{2,3},{3,2},{4,5},{5,4},{6,7},{7,6},{8,9},{9,8},{10,11... | collective-permute-start | bytes 4718600 | tf_op jit(solution)/shard_map/ppermute | solution.py:258
  229.4 5.9 %slice-start = ((s8[4718592]{0:T(1024)(128)(4,1)}), s8[4194304]{0:T(1024)(128)(4,1)S(1)}, s32[]{:S(2)}) async-start(s8[4718592]{0:T(1024)(128)(4,1)} %bitcast.60), calls=%async_computation | async-start | bytes 8388608
  233.4 12.6 %collective-permute-start.10 = (f32[6656]{0:T(1024)S(1)}, f32[6656]{0:T(1024)S(1)}, u32[]{:S(2)}, u32[]{:S(2)}) collective-permute-start(f32[6656]{0:T(1024)S(1)} %pad_maximum_fusion.6), channel_id=1, source_target_pairs={{0,1},{1,0},{2,3},{3,2},{4,5},{5,4},{6,7},{7,6},{8,9},{9,8},{10,11... | collective-permute-start | bytes 79880 | tf_op jit(solution)/shard_map/ppermute | solution.py:258
  235.3 4.0 %copy-start.29 = (bf16[2048,768]{1,0:T(8,128)(2,1)S(1)}, bf16[2048,768]{1,0:T(8,128)(2,1)}, u32[]{:S(2)}) copy-start(bf16[2048,768]{1,0:T(8,128)(2,1)} %copy-done.28) | copy-start | bytes 9437188
  246.0 3.9 %collective-permute-start.11 = (f32[6656]{0:T(1024)S(1)}, f32[6656]{0:T(1024)S(1)}, u32[]{:S(2)}, u32[]{:S(2)}) collective-permute-start(f32[6656]{0:T(1024)S(1)} %fusion.94), channel_id=1, source_target_pairs={{0,2},{1,3},{2,0},{3,1},{4,6},{5,7},{6,4},{7,5},{8,10},{9,11},{10,... | collective-permute-start | bytes 79880 | tf_op jit(solution)/shard_map/ppermute | solution.py:261
  (30 other events, 56.5 us)

commit v2 on v0

v2 whole, which is shorter than its diff:
```python
import functools
import math
import jax
import jax.numpy as jnp
from jax import lax
from jax.experimental import pallas as pl
from jax.experimental.pallas import tpu as pltpu
from jax.sharding import PartitionSpec as P

EPS = 1e-5
THETA = 10000.0
ROPE_SCALE = math.sqrt(1.0 + math.log(32.0) / math.log(4096.0))
LOG2E = math.log2(math.e)
NEG = -1e30
F32 = jnp.float32
BF16 = jnp.bfloat16


def dot(a, b):
    return lax.dot_general(a, b, (((1,), (0,)), ((), ())), preferred_element_type=F32)


def dot_nt(a, b):
    return lax.dot_general(a, b, (((1,), (1,)), ((), ())), preferred_element_type=F32)


def dot_tn(a, b):
    return lax.dot_general(a, b, (((0,), (0,)), ((), ())), preferred_element_type=F32)


def rope_tables(starts, piece, long_factor):
    half_dim = long_factor.shape[0]
    exponent = jnp.arange(half_dim, dtype=F32) * (1.0 / half_dim)
    inv_freq = 1.0 / (long_factor * THETA ** exponent)
    positions = jnp.concatenate([jnp.arange(piece, dtype=jnp.int32), starts])
    angle = positions.astype(F32)[:, None] * inv_freq[None, :]
    cos_t = jnp.cos(angle)
    sin_t = jnp.sin(angle)
    return jnp.concatenate([cos_t, cos_t], axis=1), jnp.concatenate([-sin_t, sin_t], axis=1)


def tile_tables(cos_ref, sin_ref, piece, t):
    ca = cos_ref[pl.ds(piece + t, 1), :] * ROPE_SCALE
    sa = sin_ref[pl.ds(piece + t, 1), :] * ROPE_SCALE
    cb = cos_ref[:piece, :]
    sb = sin_ref[:piece, :]
    return ca * cb - sa * sb, sa * cb + ca * sb


MESH = pl.DeviceIdType.MESH


def mega_body(nh, hd, tile, scale,
              x_hbm, d_hbm, wq_hbm, wk_hbm, wv_hbm, wo_hbm, lnw1, lnb1, bq1, bo1, bk1, bv1, cos_ref, sin_ref,
              y_hbm, dx_hbm, dwq_hbm, dwk_hbm, dwv_hbm, dwo_hbm, vec_ref,
              H, D, KV, KT, VT, WQ, WO, WKV, DK, DV, KEEP, SEND, GOT, DWT, ONA, ONS, ONR, DQA, DQS, DQR, DKA, DKS, DKR,
              DWR, VS, VR, SM, fs, fr, ns, nr, ls):
    rank = lax.axis_index('cp')
    core = rank % 2
    chip = rank // 2
    near = rank + 1 - 2 * core
    far = rank + 2 - 4 * chip
    tq = nh * tile
    qw = nh * hd
    width = H.shape[2]
    part = width // 4
    third = nh // 2
    lnw, lnb, bq, bo, bk, bv = (SM.at[n:n + 1, :] for n in range(6))
    for n, r in enumerate((lnw1, lnb1, bq1, bo1, bk1, bv1)):
        SM[n:n + 1, :r.shape[0]] = r[...].astype(F32).reshape(1, r.shape[0])

    def local(src, dst, n):
        return pltpu.make_async_copy(src, dst, ls.at[n])

    def remote(src, dst, send, recv, n, to):
        return pltpu.make_async_remote_copy(src_ref=src, dst_ref=dst, send_sem=send.at[n], recv_sem=recv.at[n],
                                            device_id={'cp': to}, device_id_type=MESH)

    def lanes_of(i, n):
        return pl.ds(pl.multiple_of(i * n, 128), n)

    def piece_of(t):
        k = t // 2
        b = (rank % 2 + k % 2) % 2 + 2 * ((rank // 2 + k // 2) % 2)
        return b + (t % 2) * (7 - 2 * b)

    def tile_of(p):
        up = p // 4
        b = p + up * (7 - 2 * p)
        k = (rank % 2 + b % 2) % 2 + 2 * ((rank // 2 + b // 2) % 2)
        return 2 * k + up

    def start_loads(X):
        mine = lanes_of(core, hd)
        return [local(x_hbm, X, 0), local(wk_hbm.at[:, mine], WKV.at[:, :hd], 1), local(wv_hbm.at[:, mine], WKV.at[:, hd:], 2),
                local(d_hbm, D.at[0:2], 3), local(wq_hbm.at[:, lanes_of(core, qw)], WQ, 4),
                local(wo_hbm.at[lanes_of(core, qw), :], WO, 5)]

    n_h = remote(H.at[0:2], H.at[2:4], ns, nr, 0, near)
    n_d = remote(D.at[0:2], D.at[2:4], ns, nr, 1, near)
    f_kv = remote(KV.at[0:4], KV.at[4:8], fs, fr, 0, far)
    f_h1 = remote(H.at[1], H.at[5], fs, fr, 1, far)
    f_d1 = remote(D.at[1], D.at[5], fs, fr, 2, far)
    f_h0 = remote(H.at[0], H.at[4], fs, fr, 3, far)
    f_d0 = remote(D.at[0], D.at[4], fs, fr, 4, far)
    n_h5 = remote(H.at[5], H.at[7], ns, nr, 2, near)
    n_d5 = remote(D.at[5], D.at[7], ns, nr, 3, near)
    n_h4 = remote(H.at[4], H.at[6], ns, nr, 4, near)
    n_d4 = remote(D.at[4], D.at[6], ns, nr, 5, near)
    n_o = remote(ONS, ONR, ns, nr, 6, near)
    n_q = remote(DQS, DQR, ns, nr, 7, near)
    n_k = remote(DKS, DKR, ns, nr, 8, near)
    n_v = remote(VS.at[0], VR.at[0], ns, nr, 10, near)
    f_v = remote(VS.at[1], VR.at[1], fs, fr, 5, far)

    def swapped(t):
        return t + 2 - 4 * ((t // 2) % 2)

    def n_s(t):
        return remote(SEND.at[t], GOT.at[swapped(t)], ns, nr, 11 + t, near)

    def n_s_in(t):
        return remote(SEND.at[swapped(t)], GOT.at[t], ns, nr, 11 + swapped(t), near)

    def head_phase(X):
        loads = start_loads(X)
        for c in loads:
            c.start()
        barrier = pltpu.get_barrier_semaphore()
        for to in (near, far):
            pl.semaphore_signal(barrier, inc=1, device_id={'cp': to}, device_id_type=MESH)
        pl.semaphore_wait(barrier, 2)
        loads[0].wait()
        gain = lnw[...]
        shift = lnb[...]

        def norm(r, _):
            rows = pl.ds(pl.multiple_of((r % 4) * 64, 64), 64)
            x = X[r // 4, rows, :].astype(F32)
            cen = x - jnp.mean(x, axis=-1, keepdims=True)
            inv = lax.rsqrt(jnp.mean(cen * cen, axis=-1, keepdims=True) + EPS)
            H[r // 4, rows, :] = (cen * inv * gain + shift).astype(BF16)
            return _

        lax.fori_loop(0, 8, norm, 0)
        n_h.start()
        loads[3].wait()
        n_d.start()
        loads[1].wait()
        loads[2].wait()
        loads[4].wait()
        loads[5].wait()

    pl.run_scoped(head_phase, pltpu.VMEM((2, tile, width), BF16))

    def attention_phase(Q, DO, PS, DPS, MS, PB, DSB, OT, DQT, DQTT):
        c = scale * LOG2E

        def rope(t, ct, st):
            t = t.astype(BF16).astype(F32)
            return (t * ct + pltpu.roll(t, hd // 2, 1) * st).astype(BF16)

        def kv_tile(t, _):
            ct, st = tile_tables(cos_ref, sin_ref, tile, t)
            kv = dot(H[t], WKV[...])
            KV[t, :, :hd] = rope(kv[:, :hd] + bk[0:1, lanes_of(core, hd)], ct, st)
            KV[t, :, hd:] = (kv[:, hd:] + bv[0:1, lanes_of(core, hd)]).astype(BF16)
            return _

        def project(t, slot):
            ct, st = tile_tables(cos_ref, sin_ref, tile, t)
            q = dot(H[t], WQ[...]) + bq[0:1, lanes_of(core, qw)]
            for n in range(nh):
                Q[slot, n] = rope(q[:, n * hd:(n + 1) * hd], ct, st)
            r = dot_nt(D[t], WO[...]).astype(BF16)
            for n in range(nh):
                DO[slot, n] = r[:, n * hd:(n + 1) * hd]

        def turn(t, _):
            KT[t] = KV[t, :, :hd].T
            VT[t] = KV[t, :, hd:].T
            return _

        lax.fori_loop(0, 2, kv_tile, 0)
        n_h.wait_recv()
        lax.fori_loop(2, 4, kv_tile, 0)
        f_kv.start()
        f_h1.start()
        f_d1.start()
        f_h0.start()
        f_d0.start()
        n_d.wait_recv()

        def first_four(t, _):
            project(t, t)
            return _

        lax.fori_loop(0, 4, first_four, 0)
        lax.fori_loop(0, 4, turn, 0)
        DK[...] = jnp.zeros_like(DK)
        DV[...] = jnp.zeros_like(DV)
        DWT[...] = jnp.zeros_like(DWT)
        f_kv.wait_recv()
        lax.fori_loop(4, 8, turn, 0)

        def one_tile(s, same):
            late = s // 4
            u = s % 4
            t = (1 - late) * ((u + 2) % 4) + late * (4 + (u % 2) * 2 + 1 - u // 2)
            slot = (1 - late) * t + late * u

            @pl.when(s == 3)
            def _():
                f_h1.wait_recv()
                f_d1.wait_recv()
                n_h5.start()
                n_d5.start()

            @pl.when(s == 5)
            def _():
                n_h5.wait_recv()
                n_d5.wait_recv()

            @pl.when(s == 6)
            def _():
                f_h0.wait_recv()
                f_d0.wait_recv()
                n_h4.start()
                n_d4.start()

            @pl.when(s == 7)
            def _():
                n_h4.wait_recv()
                n_d4.wait_recv()

            @pl.when(late == 1)
            def _():
                project(t, slot)

            i = piece_of(t)

            def first(j, carry, diag):
                m, l, dl = carry
                g = tile_of(j)
                kj = KV[g, :, :hd]
                vj = KV[g, :, hd:]
                m_new, l_new, d_new = [], [], []
                for n in range(nh):
                    lanes = slice(n * tile, (n + 1) * tile)
                    sc = dot_nt(kj, Q[slot, n]) * c
                    if diag:
                        key = lax.broadcasted_iota(jnp.int32, (tile, tile), 0)
                        qry = lax.broadcasted_iota(jnp.int32, (tile, tile), 1)
                        sc = jnp.where(key <= qry, sc, NEG)
                    dpb = dot_nt(vj, DO[slot, n]).astype(BF16)
                    DPS[j, :, lanes] = dpb
                    mo = m[:, lanes]
                    mn = jnp.maximum(mo, jnp.max(sc, axis=0, keepdims=True))
                    p = jnp.exp2(sc - mn)
                    PS[j, :, lanes] = p
                    al = jnp.exp2(mo - mn)
                    m_new.append(mn)
                    l_new.append(l[:, lanes] * al + jnp.sum(p, axis=0, keepdims=True))
                    d_new.append(dl[:, lanes] * al + jnp.sum(p * dpb.astype(F32), axis=0, keepdims=True))
                m = jnp.concatenate(m_new, axis=1)
                MS[j] = m
                return m, jnp.concatenate(l_new, axis=1), jnp.concatenate(d_new, axis=1)

            init = (jnp.full((1, tq), NEG, F32), jnp.zeros((1, tq), F32), jnp.zeros((1, tq), F32))
            carry = lax.fori_loop(0, i, lambda j, cr: first(j, cr, False), init)
            m, l, dl = first(i, carry, True)
            inv = 1.0 / l
            delta = dl * inv
            OT[...] = jnp.zeros_like(OT)
            DQT[...] = jnp.zeros_like(DQT)

            def second(j, carry):
                g = tile_of(j)
                f = jnp.exp2(MS[j] - m) * inv
                for n in range(nh):
                    lanes = slice(n * tile, (n + 1) * tile)
                    p = PS[j, :, lanes] * f[:, lanes]
                    PB[:, lanes] = p.astype(BF16)
                    DSB[:, lanes] = (p * (DPS[j, :, lanes].astype(F32) - delta[:, lanes])).astype(BF16)
                OT[...] += dot(VT[g], PB[...])
                DQT[...] += dot(KT[g], DSB[...])
                DV[g] += dot(PB[...], DO[slot].reshape(tq, hd))
                DK[g] += dot(DSB[...], Q[slot].reshape(tq, hd))
                return carry

            lax.fori_loop(0, i + 1, second, 0)
            ct, st = tile_tables(cos_ref, sin_ref, tile, t)
            cos_t = ct.T[:hd // 2]
            sin_t = st.T[hd // 2:]
            for n in range(nh):
                lanes = slice(n * tile, (n + 1) * tile)
                o_t = OT[:, lanes].astype(BF16)
                rows = slice((n % third) * hd, (n % third + 1) * hd)

                @pl.when(core == n // third)
                def _():
                    KEEP[t, rows, :] = o_t

                @pl.when(core != n // third)
                def _():
                    SEND[t, rows, :] = o_t

                gr = (DQT[:, lanes] * scale).astype(BF16).astype(F32)
                a = gr[:hd // 2]
                e = gr[hd // 2:]
                gr = jnp.concatenate([a * cos_t + e * sin_t, e * cos_t - a * sin_t], axis=0).astype(BF16)
                cols = slice(n * hd, (n + 1) * hd)
                DQTT[cols, :] = gr

                @pl.when(t // 2 == 0)
                def _():
                    ONA[t % 2, :, cols] = o_t.T
                    DQA[t % 2, :, cols] = gr.T

                @pl.when(t // 2 == 1)
                def _():
                    ONS[t % 2, :, cols] = o_t.T
                    DQS[t % 2, :, cols] = gr.T

            n_s(t).start()

            @pl.when(s == 1)
            def _():
                n_o.start()
                n_q.start()

            DWT[...] += dot(DQTT[...], H[t, :, lanes_of(chip, 2 * part)])
            return same

        lax.fori_loop(0, 8, one_tile, 0)

    pl.run_scoped(attention_phase,
                  pltpu.VMEM((4, nh, tile, hd), BF16), pltpu.VMEM((4, nh, tile, hd), BF16),
                  pltpu.VMEM((8, tile, tq), F32), pltpu.VMEM((8, tile, tq), BF16), pltpu.VMEM((8, 1, tq), F32),
                  pltpu.VMEM((tile, tq), BF16), pltpu.VMEM((tile, tq), BF16), pltpu.VMEM((hd, tq), F32), pltpu.VMEM((hd, tq), F32),
                  pltpu.VMEM((qw, tile), BF16))

    def tail_phase(DWS, X, WQO, WOO, WKVO, DKVT, DWK, DWM, ACC, AT, OUT, YB, XB):
        n_w = remote(DWS, DWR, ns, nr, 9, near)
        other = lanes_of(1 - core, hd)
        loads = [local(wq_hbm.at[:, lanes_of(1 - core, qw)], WQO, 0), local(wk_hbm.at[:, other], WKVO.at[:, :hd], 1),
                 local(wv_hbm.at[:, other], WKVO.at[:, hd:], 2), local(x_hbm, X, 3),
                 local(wo_hbm.at[lanes_of(1 - core, qw), :], WOO, 4)]
        for cp in loads:
            cp.start()

        def finish(t, same):
            ct, st = tile_tables(cos_ref, sin_ref, tile, t)
            g = (DK[t] * scale).astype(BF16).astype(F32)
            gk = (g * ct - pltpu.roll(g, hd // 2, 1) * st).astype(BF16)
            gv = DV[t].astype(BF16)
            DKVT[t, :hd, :] = gk.T
            DKVT[t, hd:, :] = gv.T

            @pl.when(t // 2 == 0)
            def _():
                DKA[t % 2, :, :hd] = gk
                DKA[t % 2, :, hd:] = gv

            @pl.when(t // 2 == 1)
            def _():
                DKS[t % 2, :, :hd] = gk
                DKS[t % 2, :, hd:] = gv

            return same

        lax.fori_loop(0, 4, finish, 0)
        n_k.start()
        lax.fori_loop(4, 8, finish, 0)

        DWK[...] = jnp.zeros_like(DWK)

        def kv_grad(t, _):
            DWK[...] += dot(DKVT[t], H[t, :, lanes_of(chip, 2 * part)])
            return _

        lax.fori_loop(0, 8, kv_grad, 0)
        theirs = lanes_of(1 - core, part)
        mine = lanes_of(core, part)
        for n in range(qw // tile):
            cols = slice(n * tile, (n + 1) * tile)
            DWS[:, cols] = DWT[cols, theirs].T
        DWS[:, qw:] = DWK[:, theirs].T
        n_w.start()
        for n in range(qw // tile):
            cols = slice(n * tile, (n + 1) * tile)
            DWM[:, cols] = DWT[cols, mine].T
        DWM[:, qw:] = DWK[:, mine].T
        outs = [local(DWM.at[:, :qw], dwq_hbm.at[:, lanes_of(core, qw)], 5),
                local(DWM.at[:, qw:qw + hd], dwk_hbm.at[:, lanes_of(core, hd)], 6),
                local(DWM.at[:, qw + hd:], dwv_hbm.at[:, lanes_of(core, hd)], 7)]
        for cp in outs:
            cp.start()

        for cp in loads[:4]:
            cp.wait()
        n_q.wait_recv()
        n_k.wait_recv()

        def rowsum(v):
            return jnp.sum(v, axis=0, keepdims=True)

        VS[0] = jnp.zeros_like(VS[0])
        gain = lnw[...]
        for t in range(2):
            ACC[...] = (dot_nt(DQA[t], WQ[...]) + dot_nt(DQR[t], WQO[...])
                        + dot_nt(DKA[t], WKV[...]) + dot_nt(DKR[t], WKVO[...]))

            def back(r, _):
                rows = pl.ds(pl.multiple_of(r * 64, 64), 64)
                dh = ACC[rows, :].astype(BF16).astype(F32)
                x = X[t, rows, :].astype(F32)
                cen = x - jnp.mean(x, axis=-1, keepdims=True)
                inv = lax.rsqrt(jnp.mean(cen * cen, axis=-1, keepdims=True) + EPS)
                xh = cen * inv
                a = dh * gain
                d = D[t, rows, :].astype(F32)
                dx = inv * (a - jnp.mean(a, axis=-1, keepdims=True) - xh * jnp.mean(a * xh, axis=-1, keepdims=True))
                XB[t, rows, :] = (d + dx).astype(BF16)
                VS[0, 0:1, :] += rowsum(dh * xh)
                VS[0, 1:2, :] += rowsum(dh)
                VS[0, 2:3, :] += rowsum(d)
                return _

            lax.fori_loop(0, tile // 64, back, 0)
            for side, q, k in ((core, DQA, DKA), (1 - core, DQR, DKR)):
                qs = rowsum(q[t].astype(F32))
                ks = rowsum(k[t].astype(F32))
                for h in range(2):
                    @pl.when(side == h)
                    def _():
                        VS[0, 3:4, h * qw:(h + 1) * qw] += qs
                        VS[0, 4:5, h * hd:(h + 1) * hd] += ks[:, :hd]
                        VS[0, 5:6, h * hd:(h + 1) * hd] += ks[:, hd:]
        n_v.start()
        outs.append(local(XB, dx_hbm, 8))
        outs[-1].start()

        loads[4].wait()
        n_o.wait_recv()
        for t in range(2):
            z = dot(ONA[t], WO[...]) + dot(ONR[t], WOO[...])
            YB[t] = (X[t].astype(F32) + (z + bo[...])).astype(BF16)
        outs.append(local(YB, y_hbm, 9))
        outs[-1].start()
        n_v.wait_recv()
        VS[1] = VS[0] + VR[0]
        f_v.start()

        def pick(t, _):
            n_s_in(t).wait_recv()
            AT[:, pl.ds(pl.multiple_of(t * tile, tile), tile)] = jnp.where(core == chip, KEEP[t], GOT[t])
            return _

        lax.fori_loop(0, 8, pick, 0)
        tn = 512
        for n in range(width // tn):
            OUT[:, n * tn:(n + 1) * tn] = dot(AT[...], D[:, :, n * tn:(n + 1) * tn].reshape(8 * tile, tn))
        outs.append(local(OUT, dwo_hbm, 10))
        outs[-1].start()
        n_w.wait_recv()
        outs += [local(DWR.at[:, :qw], dwq_hbm.at[:, lanes_of(1 - core, qw)], 11),
                 local(DWR.at[:, qw:qw + hd], dwk_hbm.at[:, lanes_of(1 - core, hd)], 12),
                 local(DWR.at[:, qw + hd:], dwv_hbm.at[:, lanes_of(1 - core, hd)], 13)]
        for cp in outs[-3:]:
            cp.start()
        f_v.wait_recv()
        vec_ref[...] = VS[1] + VR[1]
        for cp in outs:
            cp.wait()
        n_w.wait_send()

    pl.run_scoped(tail_phase,
                  pltpu.VMEM((part, qw + 2 * hd), F32), pltpu.VMEM((2, tile, width), BF16), pltpu.VMEM((width, qw), BF16), pltpu.VMEM((qw, width), BF16),
                  pltpu.VMEM((width, 2 * hd), BF16), pltpu.VMEM((8, 2 * hd, tile), BF16), pltpu.VMEM((2 * hd, 2 * part), F32),
                  pltpu.VMEM((part, qw + 2 * hd), F32), pltpu.VMEM((tile, width), F32), pltpu.VMEM((part, 8 * tile), BF16),
                  pltpu.VMEM((part, width), F32), pltpu.VMEM((2, tile, width), BF16), pltpu.VMEM((2, tile, width), BF16))

    for cp in (n_h, n_d, f_kv, f_h1, f_d1, f_h0, f_d0, n_h5, n_d5, n_h4, n_d4, n_o, n_q, n_k, n_v, f_v):
        cp.wait_send()

    def sent(t, _):
        n_s(t).wait_send()
        return _

    lax.fori_loop(0, 8, sent, 0)


def mega(x, d, wq, wk, wv, wo, small, cos_t, sin_t, nh, hd, scale):
    _, tile, width = x.shape
    qw = nh * hd
    part = width // 4
    anywhere = pl.BlockSpec(memory_space=pltpu.HBM)
    vmem = pl.BlockSpec(memory_space=pltpu.VMEM)
    rows = (2, tile, width)

    def vm(*shape, dtype=BF16):
        return pltpu.VMEM(shape, dtype)

    return pl.pallas_call(
        functools.partial(mega_body, nh, hd, tile, scale),
        in_specs=[anywhere] * 6 + [vmem] * 8,
        out_specs=[anywhere] * 6 + [vmem],
        out_shape=[jax.ShapeDtypeStruct(rows, BF16), jax.ShapeDtypeStruct(rows, BF16),
                   jax.ShapeDtypeStruct((part, 2 * qw), F32), jax.ShapeDtypeStruct((part, 2 * hd), F32),
                   jax.ShapeDtypeStruct((part, 2 * hd), F32), jax.ShapeDtypeStruct((part, width), F32),
                   jax.ShapeDtypeStruct((8, width), F32)],
        scratch_shapes=[
            vm(8, tile, width), vm(8, tile, width), vm(8, tile, 2 * hd), vm(8, hd, tile), vm(8, hd, tile),
            vm(width, qw), vm(qw, width), vm(width, 2 * hd),
            vm(8, tile, hd, dtype=F32), vm(8, tile, hd, dtype=F32),
            vm(8, part, tile), vm(8, part, tile), vm(8, part, tile), vm(qw, 2 * part, dtype=F32),
            vm(2, tile, qw), vm(2, tile, qw), vm(2, tile, qw), vm(2, tile, qw), vm(2, tile, qw), vm(2, tile, qw),
            vm(2, tile, 2 * hd), vm(2, tile, 2 * hd), vm(2, tile, 2 * hd),
            vm(part, qw + 2 * hd, dtype=F32),
            vm(2, 8, width, dtype=F32), vm(2, 8, width, dtype=F32), vm(8, width, dtype=F32),
            pltpu.SemaphoreType.DMA((6,)), pltpu.SemaphoreType.DMA((6,)),
            pltpu.SemaphoreType.DMA((19,)), pltpu.SemaphoreType.DMA((19,)), pltpu.SemaphoreType.DMA((14,))],
        compiler_params=pltpu.CompilerParams(collective_id=0, has_side_effects=True, vmem_limit_bytes=67043328),
        name="sublayer",
    )(x, d, wq, wk, wv, wo, *small, cos_t, sin_t)


def solution(mesh):
    groups = mesh.shape['cp']
    row_spec = P('dp', 'cp', None)
    mat_spec = P(('dp', 'cp'), None)
    vec_spec = P('dp')

    def device_fn(x_in, ln_w, ln_b, w_q, b_q, w_k, b_k, w_v, b_v, w_o, b_o, long_factor, dy_out):
        rank = lax.axis_index('cp').astype(jnp.int32)
        tokens, width = x_in.shape[1:]
        piece = tokens // 2
        hd = 2 * long_factor.shape[0]
        kvw = w_k.shape[1]
        nh = w_q.shape[1] // kvw
        blocks = jnp.stack([rank, rank ^ 1, rank ^ 2, rank ^ 3])
        rel = jnp.stack([blocks, 2 * groups - 1 - blocks], axis=1).reshape(2 * groups)
        cos_t, sin_t = rope_tables(rel * piece, piece, long_factor)
        small = (ln_w, ln_b, b_q, b_o, b_k, b_v)
        y, dx, d_wq, d_wk, d_wv, d_wo, vec = mega(
            x_in.reshape(2, piece, width), dy_out.reshape(2, piece, width), w_q, w_k, w_v, w_o,
            small, cos_t, sin_t, nh, hd, hd ** -0.5)
        d_lnw, d_lnb, d_bo, d_bq = (vec[n] for n in range(4))
        d_bk, d_bv = (vec[n, :kvw] for n in (4, 5))
        shape = (1, tokens, width)
        return (y.reshape(shape), dx.reshape(shape), d_wq, d_wk, d_wv, d_wo, d_lnw, d_lnb, d_bq, d_bk, d_bv, d_bo)

    in_specs = (row_spec,) + (P(),) * 11 + (row_spec,)
    out_specs = (row_spec, row_spec) + (mat_spec,) * 4 + (vec_spec,) * 6
    return jax.shard_map(device_fn, mesh=mesh, in_specs=in_specs, out_specs=out_specs, check_vma=False)
```

time: 433 us -> 154 us (0.36)
  matrix products: 223 us -> 0 us
  Pallas kernels: 0 us -> 138 us
  waiting for transfers between devices: 137 us -> 0 us
  other arithmetic: 25.1 us -> 2.25 us
  between operations: 15 us -> 0.7 us
  blocking collectives: 12.9 us -> 0 us
    dot_general x17 -> x0, matrix products: 196 us -> none  [the longest x1 50.3 us: device_fn(): jnp.einsum('tkgs,tkgd->skd', d_scores, q_groups, preferred_element_type=j...]
    pallas_call x0 -> x1, Pallas kernels: none -> 138 us  [mega(): pl.pallas_call(functools.partial(mega_body, nh, hd, tile, scale), in_spec...]
    reduce_scatter x5 -> x0, waiting for transfers between devices: 136 us -> none  [the longest x4 96.5 us: device_fn(): lax.psum_scatter(grad_mat, 'cp', scatter_dimension=0, tiled=True)]
    sub x1 -> x0, matrix products: 26.7 us -> none  [device_fn(): probs = jax.nn.softmax(jnp.where(visible, scores, -1e+30), axis=-1)]
    psum x1 -> x0, blocking collectives: 12.9 us -> none  [device_fn(): d_vecs = lax.psum((d_lnw, d_lnb, d_bq, d_bk, d_bv, d_bo), 'cp')]
    reduce_sum x6 -> x0, other arithmetic: 7.9 us -> none  [the longest x1 2.66 us: device_fn(): d_bo = jnp.sum(d_rows.astype(jnp.float32), axis=0)]
    another operation x3 -> x1, other arithmetic: 7.2 us -> 0.08 us  [device_fn(): jnp.stack([blocks, 2 * groups - 1 - blocks], axis=1).reshape(2 * groups)]
    convert_element_type x9 -> x1, other arithmetic: 4.84 us -> 0.01 us  [rope_tables(): angle = positions.astype(F32)[:, None] * inv_freq[None, :]]
  transfers between devices with their start and end apart: 6 -> 0, of which waited for: 3 -> 0; matrix products, arithmetic and copies ran while one was open for 30% -> 0% of each run, Pallas kernels for 0% -> 0%
where the time goes in v2:
time: 154 us
  Pallas kernels  138 us (90%)
  local copies, waits for them, and re-layouts  12.4 us (8%)
  other arithmetic  2.25 us (1%)
    pallas_call x1, Pallas kernels, mega(): pl.pallas_call(functools.partial(mega_body, nh, hd, tile, scale), in_spec...  138 us
    unnamed x16, local copies, waits for them, and re-layouts  9.2 us

profile of v2, /device:TPU:0, one launch (start us, length us, event | category | flops | bytes accessed | tf_op | source)
XLA Modules:
  0.0 153.6 jit_solution(1574959708269561006)
XLA Ops:
  0.6 0.7 multiply_divide_fusion
  1.3 0.1 add_bitcast_fusion
  1.4 0.1 add_subtract_fusion
  1.5 0.1 copy.26
  1.6 0.1 mul.31
  1.7 0.6 fusion
  2.2 0.8 pad_maximum_fusion
  3.1 138.3 %sublayer.1 = (bf16[2,256,1536]{2,1,0:T(8,128)(2,1)}, bf16[2,256,1536]{2,1,0:T(8,128)(2,1)}, f32[384,1536]{1,0:T(8,128)}, f32[384,256]{1,0:T(8,128)}, f32[384,25...) custom-call(bf16[2,256,1536]{2,1,0:T(8,128)(2,1)} %bitcast.18, bf16[2,256,1536]{2,1,0:T(8,128)(2,1)} %bitcast.19, ...), custom_call_target="tpu_custom_call" | custom-call | tf_op jit(solution)/shard_map/sublayer/pallas_call | solution.py:505
  141.4 0.0 copy-start.2
  141.4 1.4 fusion.1
  142.8 1.6 %slice_reduce_fusion = (f32[1536]{0:T(1024)}, f32[1536]{0:T(1024)}, f32[1536]{0:T(1024)}, f32[1536]{0:T(1024)}) fusion(f32[8,1536]{1,0:T(8,128)} %get-tuple-element.25), kind=kLoop, calls=%fused_computation.5 | loop fusion | bytes 49152 | tf_op jit(solution)/shard_map/slice | solution.py:549
  144.4 2.7 %copy.33 = bf16[1,512,1536]{2,1,0:T(8,128)(2,1)} copy(bf16[1,512,1536]{2,1,0:T(8,128)(2,1)} %bitcast.17) | data formatting | bytes 3145728
  147.1 0.0 copy-done.2
  147.1 0.0 copy-start.1
  147.1 1.1 copy.34
  148.2 1.1 copy-done.1
  149.3 0.0 copy-start.4
  149.3 0.0 copy-start.3
  149.3 0.0 copy-start
  149.3 1.4 copy.35
  150.7 0.0 copy-done.4
  150.7 0.7 copy.36
  151.5 0.0 copy-done.3
  151.5 0.7 copy.37
  152.2 0.0 copy-done
  152.2 1.4 copy.38
  (3 shorter events, 0.0 us)
Async XLA Ops:
  141.4 5.7 %copy-start.2 = (bf16[2,256,1536]{2,1,0:T(8,128)(2,1)S(1)}, bf16[2,256,1536]{2,1,0:T(8,128)(2,1)}, u32[]{:S(2)}) copy-start(bf16[2,256,1536]{2,1,0:T(8,128)(2,1)} %get-tuple-element.20) | copy-start | bytes 4718596
  147.1 2.2 %copy-start.1 = (f32[384,1536]{1,0:T(8,128)S(1)}, f32[384,1536]{1,0:T(8,128)}, u32[]{:S(2)}) copy-start(f32[384,1536]{1,0:T(8,128)} %get-tuple-element.51) | copy-start | bytes 7077892
  149.3 1.4 copy-start.4
  149.3 2.2 %copy-start.3 = (f32[384,256]{1,0:T(8,128)S(1)}, f32[384,256]{1,0:T(8,128)}, u32[]{:S(2)}) copy-start(f32[384,256]{1,0:T(8,128)} %get-tuple-element.53) | copy-start | bytes 1179652
  149.3 2.9 %copy-start = (f32[384,1536]{1,0:T(8,128)S(1)}, f32[384,1536]{1,0:T(8,128)}, u32[]{:S(2)}) copy-start(f32[384,1536]{1,0:T(8,128)} %get-tuple-element.54) | copy-start | bytes 7077892

commit v3 on v2

--- a/solution.py
+++ b/solution.py
@@ -53,7 +53,7 @@
 def mega_body(nh, hd, tile, scale,
               x_hbm, d_hbm, wq_hbm, wk_hbm, wv_hbm, wo_hbm, lnw1, lnb1, bq1, bo1, bk1, bv1, cos_ref, sin_ref,
               y_hbm, dx_hbm, dwq_hbm, dwk_hbm, dwv_hbm, dwo_hbm, vec_ref,
-              H, D, KV, KT, VT, WQ, WO, WKV, DK, DV, KEEP, SEND, GOT, DWT, ONA, ONS, ONR, DQA, DQS, DQR, DKA, DKS, DKR,
+              H, D, KV, KT, VT, WQ, WO, WKV, DK, DV, AT, SEND, DWT, ONA, ONS, ONR, DQA, DQS, DQR, DKA, DKS, DKR,
               DWR, VS, VR, SM, fs, fr, ns, nr, ls):
     rank = lax.axis_index('cp')
     core = rank % 2
@@ -98,9 +98,11 @@
 
     n_h = remote(H.at[0:2], H.at[2:4], ns, nr, 0, near)
     n_d = remote(D.at[0:2], D.at[2:4], ns, nr, 1, near)
-    f_kv = remote(KV.at[0:4], KV.at[4:8], fs, fr, 0, far)
+    f_kv = remote(KV.at[0:2], KV.at[4:6], fs, fr, 0, far)
+    f_kw = remote(KV.at[2:4], KV.at[6:8], fs, fr, 6, far)
     f_h1 = remote(H.at[1], H.at[5], fs, fr, 1, far)
-    f_d1 = remote(D.at[1], D.at[5], fs, fr, 2, far)
+    f_d1 = remote(D.at[1, :tile // 2], D.at[5, :tile // 2], fs, fr, 2, far)
+    f_e1 = remote(D.at[1, tile // 2:], D.at[5, tile // 2:], fs, fr, 7, far)
     f_h0 = remote(H.at[0], H.at[4], fs, fr, 3, far)
     f_d0 = remote(D.at[0], D.at[4], fs, fr, 4, far)
     n_h5 = remote(H.at[5], H.at[7], ns, nr, 2, near)
@@ -116,11 +118,18 @@
     def swapped(t):
         return t + 2 - 4 * ((t // 2) % 2)
 
-    def n_s(t):
-        return remote(SEND.at[t], GOT.at[swapped(t)], ns, nr, 11 + t, near)
+    holds = core == chip
+
+    def n_s(t, s):
+        return remote(SEND.at[s % 2], AT.at[swapped(t)], ns, nr, 11 + t, near)
 
     def n_s_in(t):
-        return remote(SEND.at[swapped(t)], GOT.at[t], ns, nr, 11 + swapped(t), near)
+        return remote(SEND.at[0], AT.at[t], ns, nr, 11 + swapped(t), near)
+
+    def tile_at(s):
+        late = s // 4
+        u = s % 4
+        return (1 - late) * ((u + 2) % 4) + late * (4 + (u % 2) * 2 + 1 - u // 2)
 
     def head_phase(X):
         loads = start_loads(X)
@@ -130,6 +139,8 @@
         for to in (near, far):
             pl.semaphore_signal(barrier, inc=1, device_id={'cp': to}, device_id_type=MESH)
         pl.semaphore_wait(barrier, 2)
+        loads[3].wait()
+        f_d1.start()
         loads[0].wait()
         gain = lnw[...]
         shift = lnb[...]
@@ -144,7 +155,6 @@
 
         lax.fori_loop(0, 8, norm, 0)
         n_h.start()
-        loads[3].wait()
         n_d.start()
         loads[1].wait()
         loads[2].wait()
@@ -182,11 +192,12 @@
             return _
 
         lax.fori_loop(0, 2, kv_tile, 0)
+        f_kv.start()
         n_h.wait_recv()
         lax.fori_loop(2, 4, kv_tile, 0)
-        f_kv.start()
+        f_kw.start()
         f_h1.start()
-        f_d1.start()
+        f_e1.start()
         f_h0.start()
         f_d0.start()
         n_d.wait_recv()
@@ -201,18 +212,21 @@
         DV[...] = jnp.zeros_like(DV)
         DWT[...] = jnp.zeros_like(DWT)
         f_kv.wait_recv()
-        lax.fori_loop(4, 8, turn, 0)
+        lax.fori_loop(4, 6, turn, 0)
+        f_kw.wait_recv()
+        lax.fori_loop(6, 8, turn, 0)
 
         def one_tile(s, same):
             late = s // 4
             u = s % 4
-            t = (1 - late) * ((u + 2) % 4) + late * (4 + (u % 2) * 2 + 1 - u // 2)
+            t = tile_at(s)
             slot = (1 - late) * t + late * u
 
-            @pl.when(s == 3)
+            @pl.when(s == 4)
             def _():
                 f_h1.wait_recv()
                 f_d1.wait_recv()
+                f_e1.wait_recv()
                 n_h5.start()
                 n_d5.start()
 
@@ -267,43 +281,61 @@
                 return m, jnp.concatenate(l_new, axis=1), jnp.concatenate(d_new, axis=1)
 
             init = (jnp.full((1, tq), NEG, F32), jnp.zeros((1, tq), F32), jnp.zeros((1, tq), F32))
-            carry = lax.fori_loop(0, i, lambda j, cr: first(j, cr, False), init)
+            carry = lax.fori_loop(0, i // 2, lambda h, cr: first(2 * h + 1, first(2 * h, cr, False), False), init)
+            carry = lax.fori_loop(2 * (i // 2), i, lambda j, cr: first(j, cr, False), carry)
             m, l, dl = first(i, carry, True)
             inv = 1.0 / l
             delta = dl * inv
             OT[...] = jnp.zeros_like(OT)
             DQT[...] = jnp.zeros_like(DQT)
 
-            def second(j, carry):
-                g = tile_of(j)
+            def weigh(j, k):
                 f = jnp.exp2(MS[j] - m) * inv
                 for n in range(nh):
                     lanes = slice(n * tile, (n + 1) * tile)
                     p = PS[j, :, lanes] * f[:, lanes]
-                    PB[:, lanes] = p.astype(BF16)
-                    DSB[:, lanes] = (p * (DPS[j, :, lanes].astype(F32) - delta[:, lanes])).astype(BF16)
-                OT[...] += dot(VT[g], PB[...])
-                DQT[...] += dot(KT[g], DSB[...])
-                DV[g] += dot(PB[...], DO[slot].reshape(tq, hd))
-                DK[g] += dot(DSB[...], Q[slot].reshape(tq, hd))
+                    PB[k, :, lanes] = p.astype(BF16)
+                    DSB[k, :, lanes] = (p * (DPS[j, :, lanes].astype(F32) - delta[:, lanes])).astype(BF16)
+
+            def second(js, carry):
+                gs = [tile_of(j) for j in js]
+                for k, j in enumerate(js):
+                    weigh(j, k)
+                o = dot(VT[gs[0]], PB[0])
+                dq = dot(KT[gs[0]], DSB[0])
+                for k in range(1, len(js)):
+                    o += dot(VT[gs[k]], PB[k])
+                    dq += dot(KT[gs[k]], DSB[k])
+                OT[...] += o
+                DQT[...] += dq
+                for k, g in enumerate(gs):
+                    DV[g] += dot(PB[k], DO[slot].reshape(tq, hd))
+                    DK[g] += dot(DSB[k], Q[slot].reshape(tq, hd))
                 return carry
 
-            lax.fori_loop(0, i + 1, second, 0)
+            pairs = (i + 1) // 2
+            lax.fori_loop(0, pairs, lambda h, cr: second((2 * h, 2 * h + 1), cr), 0)
+            lax.fori_loop(2 * pairs, i + 1, lambda j, cr: second((j,), cr), 0)
             ct, st = tile_tables(cos_ref, sin_ref, tile, t)
             cos_t = ct.T[:hd // 2]
+
+            @pl.when(jnp.logical_and(holds, s >= 2))
+            def _():
+                n_s(tile_at(s - 2), s).wait_send()
+
             sin_t = st.T[hd // 2:]
             for n in range(nh):
                 lanes = slice(n * tile, (n + 1) * tile)
                 o_t = OT[:, lanes].astype(BF16)
                 rows = slice((n % third) * hd, (n % third + 1) * hd)
 
-                @pl.when(core == n // third)
+                @pl.when(jnp.logical_and(holds, core == n // third))
                 def _():
-                    KEEP[t, rows, :] = o_t
-
-                @pl.when(core != n // third)
+                    AT[t, rows, :] = o_t
+
+                @pl.when(jnp.logical_and(holds, core != n // third))
                 def _():
-                    SEND[t, rows, :] = o_t
+                    SEND[s % 2, rows, :] = o_t
 
                 gr = (DQT[:, lanes] * scale).astype(BF16).astype(F32)
                 a = gr[:hd // 2]
@@ -322,7 +354,9 @@
                     ONS[t % 2, :, cols] = o_t.T
                     DQS[t % 2, :, cols] = gr.T
 
-            n_s(t).start()
+            @pl.when(holds)
+            def _():
+                n_s(t, s).start()
 
             @pl.when(s == 1)
             def _():
@@ -337,10 +371,10 @@
     pl.run_scoped(attention_phase,
                   pltpu.VMEM((4, nh, tile, hd), BF16), pltpu.VMEM((4, nh, tile, hd), BF16),
                   pltpu.VMEM((8, tile, tq), F32), pltpu.VMEM((8, tile, tq), BF16), pltpu.VMEM((8, 1, tq), F32),
-                  pltpu.VMEM((tile, tq), BF16), pltpu.VMEM((tile, tq), BF16), pltpu.VMEM((hd, tq), F32), pltpu.VMEM((hd, tq), F32),
+                  pltpu.VMEM((2, tile, tq), BF16), pltpu.VMEM((2, tile, tq), BF16), pltpu.VMEM((hd, tq), F32), pltpu.VMEM((hd, tq), F32),
                   pltpu.VMEM((qw, tile), BF16))
 
-    def tail_phase(DWS, X, WQO, WOO, WKVO, DKVT, DWK, DWM, ACC, AT, OUT, YB, XB):
+    def tail_phase(DWS, X, WQO, WOO, WKVO, DKVT, DWK, DWM, ACC, OUT, YB, XB):
         n_w = remote(DWS, DWR, ns, nr, 9, near)
         other = lanes_of(1 - core, hd)
         loads = [local(wq_hbm.at[:, lanes_of(1 - core, qw)], WQO, 0), local(wk_hbm.at[:, other], WKVO.at[:, :hd], 1),
@@ -452,15 +486,18 @@
         VS[1] = VS[0] + VR[0]
         f_v.start()
 
-        def pick(t, _):
-            n_s_in(t).wait_recv()
-            AT[:, pl.ds(pl.multiple_of(t * tile, tile), tile)] = jnp.where(core == chip, KEEP[t], GOT[t])
-            return _
-
-        lax.fori_loop(0, 8, pick, 0)
+        @pl.when(jnp.logical_not(holds))
+        def _():
+            for t in range(8):
+                n_s_in(t).wait_recv()
+
         tn = 512
         for n in range(width // tn):
-            OUT[:, n * tn:(n + 1) * tn] = dot(AT[...], D[:, :, n * tn:(n + 1) * tn].reshape(8 * tile, tn))
+            cols = slice(n * tn, (n + 1) * tn)
+            acc = dot(AT[0], D[0, :, cols])
+            for t in range(1, 8):
+                acc += dot(AT[t], D[t, :, cols])
+            OUT[:, cols] = acc
         outs.append(local(OUT, dwo_hbm, 10))
         outs[-1].start()
         n_w.wait_recv()
@@ -478,17 +515,16 @@
     pl.run_scoped(tail_phase,
                   pltpu.VMEM((part, qw + 2 * hd), F32), pltpu.VMEM((2, tile, width), BF16), pltpu.VMEM((width, qw), BF16), pltpu.VMEM((qw, width), BF16),
                   pltpu.VMEM((width, 2 * hd), BF16), pltpu.VMEM((8, 2 * hd, tile), BF16), pltpu.VMEM((2 * hd, 2 * part), F32),
-                  pltpu.VMEM((part, qw + 2 * hd), F32), pltpu.VMEM((tile, width), F32), pltpu.VMEM((part, 8 * tile), BF16),
+                  pltpu.VMEM((part, qw + 2 * hd), F32), pltpu.VMEM((tile, width), F32),
                   pltpu.VMEM((part, width), F32), pltpu.VMEM((2, tile, width), BF16), pltpu.VMEM((2, tile, width), BF16))
 
-    for cp in (n_h, n_d, f_kv, f_h1, f_d1, f_h0, f_d0, n_h5, n_d5, n_h4, n_d4, n_o, n_q, n_k, n_v, f_v):
+    for cp in (n_h, n_d, f_kv, f_kw, f_h1, f_d1, f_e1, f_h0, f_d0, n_h5, n_d5, n_h4, n_d4, n_o, n_q, n_k, n_v, f_v):
         cp.wait_send()
 
-    def sent(t, _):
-        n_s(t).wait_send()
-        return _
-
-    lax.fori_loop(0, 8, sent, 0)
+    @pl.when(holds)
+    def _():
+        for s in (6, 7):
+            n_s(tile_at(s), s).wait_send()
 
 
 def mega(x, d, wq, wk, wv, wo, small, cos_t, sin_t, nh, hd, scale):
@@ -514,12 +550,12 @@
             vm(8, tile, width), vm(8, tile, width), vm(8, tile, 2 * hd), vm(8, hd, tile), vm(8, hd, tile),
             vm(width, qw), vm(qw, width), vm(width, 2 * hd),
             vm(8, tile, hd, dtype=F32), vm(8, tile, hd, dtype=F32),
-            vm(8, part, tile), vm(8, part, tile), vm(8, part, tile), vm(qw, 2 * part, dtype=F32),
+            vm(8, part, tile), vm(2, part, tile), vm(qw, 2 * part, dtype=F32),
             vm(2, tile, qw), vm(2, tile, qw), vm(2, tile, qw), vm(2, tile, qw), vm(2, tile, qw), vm(2, tile, qw),
             vm(2, tile, 2 * hd), vm(2, tile, 2 * hd), vm(2, tile, 2 * hd),
             vm(part, qw + 2 * hd, dtype=F32),
             vm(2, 8, width, dtype=F32), vm(2, 8, width, dtype=F32), vm(8, width, dtype=F32),
-            pltpu.SemaphoreType.DMA((6,)), pltpu.SemaphoreType.DMA((6,)),
+            pltpu.SemaphoreType.DMA((8,)), pltpu.SemaphoreType.DMA((8,)),
             pltpu.SemaphoreType.DMA((19,)), pltpu.SemaphoreType.DMA((19,)), pltpu.SemaphoreType.DMA((14,))],
         compiler_params=pltpu.CompilerParams(collective_id=0, has_side_effects=True, vmem_limit_bytes=67043328),
         name="sublayer",

time: 154 us -> 144 us (0.935)
  Pallas kernels: 138 us -> 128 us
    pallas_call x1, Pallas kernels: 138 us -> 128 us  [mega(): pl.pallas_call(functools.partial(mega_body, nh, hd, tile, scale), in_spec...]
where the time goes in v3:
time: 144 us; the launch traced here: 143 us
  Pallas kernels  128 us (89%)
  local copies, waits for them, and re-layouts  12.4 us (9%)
  other arithmetic  2.25 us (2%)
    pallas_call x1, Pallas kernels, mega(): pl.pallas_call(functools.partial(mega_body, nh, hd, tile, scale), in_spec...  128 us
    unnamed x16, local copies, waits for them, and re-layouts  9.2 us

profile of v3, /device:TPU:0, one launch (start us, length us, event | category | flops | bytes accessed | tf_op | source)
XLA Modules:
  0.0 143.4 jit_solution(17179616757803806434)
XLA Ops:
  0.6 0.7 multiply_divide_fusion
  1.3 0.1 add_bitcast_fusion
  1.4 0.1 add_subtract_fusion
  1.5 0.1 copy.26
  1.6 0.1 mul.31
  1.7 0.6 fusion
  2.2 0.8 pad_maximum_fusion
  3.1 128.0 %sublayer.1 = (bf16[2,256,1536]{2,1,0:T(8,128)(2,1)}, bf16[2,256,1536]{2,1,0:T(8,128)(2,1)}, f32[384,1536]{1,0:T(8,128)}, f32[384,256]{1,0:T(8,128)}, f32[384,25...) custom-call(bf16[2,256,1536]{2,1,0:T(8,128)(2,1)} %bitcast.18, bf16[2,256,1536]{2,1,0:T(8,128)(2,1)} %bitcast.19, ...), custom_call_target="tpu_custom_call" | custom-call | tf_op jit(solution)/shard_map/sublayer/pallas_call | solution.py:541
  131.1 0.0 copy-start.2
  131.1 1.4 fusion.1
  132.5 1.6 %slice_reduce_fusion = (f32[1536]{0:T(1024)}, f32[1536]{0:T(1024)}, f32[1536]{0:T(1024)}, f32[1536]{0:T(1024)}) fusion(f32[8,1536]{1,0:T(8,128)} %get-tuple-element.25), kind=kLoop, calls=%fused_computation.5 | loop fusion | bytes 49152 | tf_op jit(solution)/shard_map/slice | solution.py:585
  134.2 2.7 %copy.33 = bf16[1,512,1536]{2,1,0:T(8,128)(2,1)} copy(bf16[1,512,1536]{2,1,0:T(8,128)(2,1)} %bitcast.17) | data formatting | bytes 3145728
  136.8 0.0 copy-done.2
  136.8 0.0 copy-start.1
  136.8 1.1 copy.34
  138.0 1.1 copy-done.1
  139.0 0.0 copy-start.4
  139.0 0.0 copy-start.3
  139.1 0.0 copy-start
  139.1 1.4 copy.35
  140.5 0.0 copy-done.4
  140.5 0.7 copy.36
  141.2 0.0 copy-done.3
  141.2 0.7 copy.37
  142.0 0.0 copy-done
  142.0 1.4 copy.38
  (3 shorter events, 0.0 us)
Async XLA Ops:
  131.1 5.7 %copy-start.2 = (bf16[2,256,1536]{2,1,0:T(8,128)(2,1)S(1)}, bf16[2,256,1536]{2,1,0:T(8,128)(2,1)}, u32[]{:S(2)}) copy-start(bf16[2,256,1536]{2,1,0:T(8,128)(2,1)} %get-tuple-element.20) | copy-start | bytes 4718596
  136.8 2.2 %copy-start.1 = (f32[384,1536]{1,0:T(8,128)S(1)}, f32[384,1536]{1,0:T(8,128)}, u32[]{:S(2)}) copy-start(f32[384,1536]{1,0:T(8,128)} %get-tuple-element.51) | copy-start | bytes 7077892
  139.0 1.4 copy-start.4
  139.0 2.2 %copy-start.3 = (f32[384,256]{1,0:T(8,128)S(1)}, f32[384,256]{1,0:T(8,128)}, u32[]{:S(2)}) copy-start(f32[384,256]{1,0:T(8,128)} %get-tuple-element.53) | copy-start | bytes 1179652
  139.1 2.9 %copy-start = (f32[384,1536]{1,0:T(8,128)S(1)}, f32[384,1536]{1,0:T(8,128)}, u32[]{:S(2)}) copy-start(f32[384,1536]{1,0:T(8,128)} %get-tuple-element.54) | copy-start | bytes 7077892

commit v4 on v3

--- a/solution.py
+++ b/solution.py
@@ -52,9 +52,9 @@
 
 def mega_body(nh, hd, tile, scale,
               x_hbm, d_hbm, wq_hbm, wk_hbm, wv_hbm, wo_hbm, lnw1, lnb1, bq1, bo1, bk1, bv1, cos_ref, sin_ref,
-              y_hbm, dx_hbm, dwq_hbm, dwk_hbm, dwv_hbm, dwo_hbm, vec_ref,
+              y_hbm, dx_hbm, dwm_hbm, DWR, dwo_hbm, vec_ref,
               H, D, KV, KT, VT, WQ, WO, WKV, DK, DV, AT, SEND, DWT, ONA, ONS, ONR, DQA, DQS, DQR, DKA, DKS, DKR,
-              DWR, VS, VR, SM, fs, fr, ns, nr, ls):
+              VS, VR, SM, fs, fr, ns, nr, ls):
     rank = lax.axis_index('cp')
     core = rank % 2
     chip = rank // 2
@@ -416,96 +416,83 @@
         lax.fori_loop(0, 8, kv_grad, 0)
         theirs = lanes_of(1 - core, part)
         mine = lanes_of(core, part)
-        for n in range(qw // tile):
-            cols = slice(n * tile, (n + 1) * tile)
-            DWS[:, cols] = DWT[cols, theirs].T
-        DWS[:, qw:] = DWK[:, theirs].T
-        n_w.start()
-        for n in range(qw // tile):
-            cols = slice(n * tile, (n + 1) * tile)
-            DWM[:, cols] = DWT[cols, mine].T
-        DWM[:, qw:] = DWK[:, mine].T
-        outs = [local(DWM.at[:, :qw], dwq_hbm.at[:, lanes_of(core, qw)], 5),
-                local(DWM.at[:, qw:qw + hd], dwk_hbm.at[:, lanes_of(core, hd)], 6),
-                local(DWM.at[:, qw + hd:], dwv_hbm.at[:, lanes_of(core, hd)], 7)]
-        for cp in outs:
-            cp.start()
-
         for cp in loads[:4]:
             cp.wait()
         n_q.wait_recv()
         n_k.wait_recv()
-
-        def rowsum(v):
-            return jnp.sum(v, axis=0, keepdims=True)
-
-        VS[0] = jnp.zeros_like(VS[0])
-        gain = lnw[...]
         for t in range(2):
-            ACC[...] = (dot_nt(DQA[t], WQ[...]) + dot_nt(DQR[t], WQO[...])
-                        + dot_nt(DKA[t], WKV[...]) + dot_nt(DKR[t], WKVO[...]))
-
-            def back(r, _):
-                rows = pl.ds(pl.multiple_of(r * 64, 64), 64)
-                dh = ACC[rows, :].astype(BF16).astype(F32)
-                x = X[t, rows, :].astype(F32)
-                cen = x - jnp.mean(x, axis=-1, keepdims=True)
-                inv = lax.rsqrt(jnp.mean(cen * cen, axis=-1, keepdims=True) + EPS)
-                xh = cen * inv
-                a = dh * gain
-                d = D[t, rows, :].astype(F32)
-                dx = inv * (a - jnp.mean(a, axis=-1, keepdims=True) - xh * jnp.mean(a * xh, axis=-1, keepdims=True))
-                XB[t, rows, :] = (d + dx).astype(BF16)
-                VS[0, 0:1, :] += rowsum(dh * xh)
-                VS[0, 1:2, :] += rowsum(dh)
-                VS[0, 2:3, :] += rowsum(d)
-                return _
-
-            lax.fori_loop(0, tile // 64, back, 0)
-            for side, q, k in ((core, DQA, DKA), (1 - core, DQR, DKR)):
-                qs = rowsum(q[t].astype(F32))
-                ks = rowsum(k[t].astype(F32))
-                for h in range(2):
-                    @pl.when(side == h)
-                    def _():
-                        VS[0, 3:4, h * qw:(h + 1) * qw] += qs
-                        VS[0, 4:5, h * hd:(h + 1) * hd] += ks[:, :hd]
-                        VS[0, 5:6, h * hd:(h + 1) * hd] += ks[:, hd:]
-        n_v.start()
-        outs.append(local(XB, dx_hbm, 8))
-        outs[-1].start()
-
-        loads[4].wait()
-        n_o.wait_recv()
-        for t in range(2):
-            z = dot(ONA[t], WO[...]) + dot(ONR[t], WOO[...])
-            YB[t] = (X[t].astype(F32) + (z + bo[...])).astype(BF16)
-        outs.append(local(YB, y_hbm, 9))
-        outs[-1].start()
-        n_v.wait_recv()
-        VS[1] = VS[0] + VR[0]
-        f_v.start()
+            ACC[t * tile:(t + 1) * tile, :] = (dot_nt(DQA[t], WQ[...]) + dot_nt(DQR[t], WQO[...])
+                                               + dot_nt(DKA[t], WKV[...]) + dot_nt(DKR[t], WKVO[...]))
+        for cols_of, out in ((theirs, DWS), (mine, DWM)):
+            for n in range(qw // tile):
+                cols = slice(n * tile, (n + 1) * tile)
+                out[:, cols] = DWT[cols, cols_of].T
+            out[:, qw:] = DWK[:, cols_of].T
+        n_w.start()
+        outs = [local(DWM, dwm_hbm, 5)]
+        outs[0].start()
 
         @pl.when(jnp.logical_not(holds))
         def _():
             for t in range(8):
                 n_s_in(t).wait_recv()
 
-        tn = 512
-        for n in range(width // tn):
-            cols = slice(n * tn, (n + 1) * tn)
-            acc = dot(AT[0], D[0, :, cols])
+        def rowsum(v):
+            return jnp.sum(v, axis=0, keepdims=True)
+
+        VS[0] = jnp.zeros_like(VS[0])
+        gain = lnw[...]
+        chunk = tile // 2
+        tn = width // 4
+
+        def back(r, same):
+            lanes = lanes_of(r, tn)
+            acc = dot(AT[0], D[0, :, lanes])
             for t in range(1, 8):
-                acc += dot(AT[t], D[t, :, cols])
-            OUT[:, cols] = acc
-        outs.append(local(OUT, dwo_hbm, 10))
+                acc += dot(AT[t], D[t, :, lanes])
+            OUT[:, lanes] = acc
+            rows = pl.ds(pl.multiple_of((r % 2) * chunk, chunk), chunk)
+            dh = ACC[pl.ds(pl.multiple_of(r * chunk, chunk), chunk), :].astype(BF16).astype(F32)
+            x = X[r // 2, rows, :].astype(F32)
+            cen = x - jnp.mean(x, axis=-1, keepdims=True)
+            inv = lax.rsqrt(jnp.mean(cen * cen, axis=-1, keepdims=True) + EPS)
+            xh = cen * inv
+            a = dh * gain
+            d = D[r // 2, rows, :].astype(F32)
+            dx = inv * (a - jnp.mean(a, axis=-1, keepdims=True) - xh * jnp.mean(a * xh, axis=-1, keepdims=True))
+            XB[r // 2, rows, :] = (d + dx).astype(BF16)
+            VS[0, 0:1, :] += rowsum(dh * xh)
+            VS[0, 1:2, :] += rowsum(dh)
+            VS[0, 2:3, :] += rowsum(d)
+            return same
+
+        lax.fori_loop(0, 4, back, 0)
+        for side, q, k in ((core, DQA, DKA), (1 - core, DQR, DKR)):
+            qs = rowsum(q[0].astype(F32)) + rowsum(q[1].astype(F32))
+            ks = rowsum(k[0].astype(F32)) + rowsum(k[1].astype(F32))
+            VS[0, 3:4, lanes_of(side, qw)] = qs
+            VS[0, 4:5, lanes_of(side, hd)] = ks[:, :hd]
+            VS[0, 5:6, lanes_of(side, hd)] = ks[:, hd:]
+        n_v.start()
+        outs += [local(XB, dx_hbm, 8), local(OUT, dwo_hbm, 10)]
+        outs[1].start()
+        outs[2].start()
+
+        loads[4].wait()
+        n_o.wait_recv()
+
+        def y_tile(t):
+            z = dot(ONA[t], WO[...]) + dot(ONR[t], WOO[...])
+            YB[t] = (X[t].astype(F32) + (z + bo[...])).astype(BF16)
+
+        y_tile(0)
+        n_v.wait_recv()
+        VS[1] = VS[0] + VR[0]
+        f_v.start()
+        y_tile(1)
+        outs.append(local(YB, y_hbm, 9))
         outs[-1].start()
         n_w.wait_recv()
-        outs += [local(DWR.at[:, :qw], dwq_hbm.at[:, lanes_of(1 - core, qw)], 11),
-                 local(DWR.at[:, qw:qw + hd], dwk_hbm.at[:, lanes_of(1 - core, hd)], 12),
-                 local(DWR.at[:, qw + hd:], dwv_hbm.at[:, lanes_of(1 - core, hd)], 13)]
-        for cp in outs[-3:]:
-            cp.start()
         f_v.wait_recv()
         vec_ref[...] = VS[1] + VR[1]
         for cp in outs:
@@ -515,7 +502,7 @@
     pl.run_scoped(tail_phase,
                   pltpu.VMEM((part, qw + 2 * hd), F32), pltpu.VMEM((2, tile, width), BF16), pltpu.VMEM((width, qw), BF16), pltpu.VMEM((qw, width), BF16),
                   pltpu.VMEM((width, 2 * hd), BF16), pltpu.VMEM((8, 2 * hd, tile), BF16), pltpu.VMEM((2 * hd, 2 * part), F32),
-                  pltpu.VMEM((part, qw + 2 * hd), F32), pltpu.VMEM((tile, width), F32),
+                  pltpu.VMEM((part, qw + 2 * hd), F32), pltpu.VMEM((2 * tile, width), F32),
                   pltpu.VMEM((part, width), F32), pltpu.VMEM((2, tile, width), BF16), pltpu.VMEM((2, tile, width), BF16))
 
     for cp in (n_h, n_d, f_kv, f_kw, f_h1, f_d1, f_e1, f_h0, f_d0, n_h5, n_d5, n_h4, n_d4, n_o, n_q, n_k, n_v, f_v):
@@ -541,10 +528,10 @@
     return pl.pallas_call(
         functools.partial(mega_body, nh, hd, tile, scale),
         in_specs=[anywhere] * 6 + [vmem] * 8,
-        out_specs=[anywhere] * 6 + [vmem],
+        out_specs=[anywhere] * 5 + [vmem],
         out_shape=[jax.ShapeDtypeStruct(rows, BF16), jax.ShapeDtypeStruct(rows, BF16),
-                   jax.ShapeDtypeStruct((part, 2 * qw), F32), jax.ShapeDtypeStruct((part, 2 * hd), F32),
-                   jax.ShapeDtypeStruct((part, 2 * hd), F32), jax.ShapeDtypeStruct((part, width), F32),
+                   jax.ShapeDtypeStruct((part, qw + 2 * hd), F32), jax.ShapeDtypeStruct((part, qw + 2 * hd), F32),
+                   jax.ShapeDtypeStruct((part, width), F32),
                    jax.ShapeDtypeStruct((8, width), F32)],
         scratch_shapes=[
             vm(8, tile, width), vm(8, tile, width), vm(8, tile, 2 * hd), vm(8, hd, tile), vm(8, hd, tile),
@@ -553,13 +540,53 @@
             vm(8, part, tile), vm(2, part, tile), vm(qw, 2 * part, dtype=F32),
             vm(2, tile, qw), vm(2, tile, qw), vm(2, tile, qw), vm(2, tile, qw), vm(2, tile, qw), vm(2, tile, qw),
             vm(2, tile, 2 * hd), vm(2, tile, 2 * hd), vm(2, tile, 2 * hd),
-            vm(part, qw + 2 * hd, dtype=F32),
             vm(2, 8, width, dtype=F32), vm(2, 8, width, dtype=F32), vm(8, width, dtype=F32),
             pltpu.SemaphoreType.DMA((8,)), pltpu.SemaphoreType.DMA((8,)),
             pltpu.SemaphoreType.DMA((19,)), pltpu.SemaphoreType.DMA((19,)), pltpu.SemaphoreType.DMA((14,))],
         compiler_params=pltpu.CompilerParams(collective_id=0, has_side_effects=True, vmem_limit_bytes=67043328),
         name="sublayer",
     )(x, d, wq, wk, wv, wo, *small, cos_t, sin_t)
+
+
+def finish_body(hd, c_ref, y_ref, dx_ref, m_ref, t_ref, o_ref, v_ref, y_out, dx_out, q_out, k_out, v_out, o_out, *vecs):
+    core = c_ref[0]
+    y_out[...] = y_ref[...]
+    dx_out[...] = dx_ref[...]
+    o_out[...] = o_ref[...]
+    qw = q_out.shape[1] // 2
+    for side, r in ((core, m_ref), (1 - core, t_ref)):
+        q_out[:, pl.ds(pl.multiple_of(side * qw, 128), qw)] = r[:, :qw]
+        k_out[:, pl.ds(pl.multiple_of(side * hd, 128), hd)] = r[:, qw:qw + hd]
+        v_out[:, pl.ds(pl.multiple_of(side * hd, 128), hd)] = r[:, qw + hd:]
+
+    @pl.when(pl.program_id(0) == 0)
+    def _():
+        for n, r in enumerate(vecs):
+            r[...] = v_ref[n:n + 1, :r.shape[0]].reshape(r.shape[0])
+
+
+def finish(core, y, dx, mine, theirs, d_wo, vec, hd, kvw, steps=4):
+    rows, width = y.shape
+    part, cols = mine.shape
+    qw = cols - 2 * hd
+
+    def tall(r, c):
+        return pl.BlockSpec((r // steps, c), lambda i, s: (i, 0))
+
+    dims = [(rows, width), (rows, width), (part, 2 * qw), (part, 2 * hd), (part, 2 * hd), (part, width)]
+    lens = [width] * 4 + [kvw] * 2
+    return pl.pallas_call(
+        functools.partial(finish_body, hd),
+        grid_spec=pltpu.PrefetchScalarGridSpec(
+            num_scalar_prefetch=1, grid=(steps,),
+            in_specs=[tall(rows, width), tall(rows, width), tall(part, cols), tall(part, cols), tall(part, width),
+                      pl.BlockSpec(vec.shape, lambda i, s: (0, 0))],
+            out_specs=[tall(*d) for d in dims] + [pl.BlockSpec((n,), lambda i, s: (0,)) for n in lens]),
+        out_shape=[jax.ShapeDtypeStruct(d, BF16 if n < 2 else F32) for n, d in enumerate(dims)]
+        + [jax.ShapeDtypeStruct((n,), F32) for n in lens],
+        compiler_params=pltpu.CompilerParams(dimension_semantics=("arbitrary",), vmem_limit_bytes=67043328),
+        name="finish",
+    )(core, y, dx, mine, theirs, d_wo, vec)
 
 
 def solution(mesh):
@@ -579,11 +606,11 @@
         rel = jnp.stack([blocks, 2 * groups - 1 - blocks], axis=1).reshape(2 * groups)
         cos_t, sin_t = rope_tables(rel * piece, piece, long_factor)
         small = (ln_w, ln_b, b_q, b_o, b_k, b_v)
-        y, dx, d_wq, d_wk, d_wv, d_wo, vec = mega(
+        y, dx, mine, theirs, d_wo, vec = mega(
             x_in.reshape(2, piece, width), dy_out.reshape(2, piece, width), w_q, w_k, w_v, w_o,
             small, cos_t, sin_t, nh, hd, hd ** -0.5)
-        d_lnw, d_lnb, d_bo, d_bq = (vec[n] for n in range(4))
-        d_bk, d_bv = (vec[n, :kvw] for n in (4, 5))
+        y, dx, d_wq, d_wk, d_wv, d_wo, d_lnw, d_lnb, d_bo, d_bq, d_bk, d_bv = finish(
+            (rank % 2)[None], y.reshape(tokens, width), dx.reshape(tokens, width), mine, theirs, d_wo, vec, hd, kvw)
         shape = (1, tokens, width)
         return (y.reshape(shape), dx.reshape(shape), d_wq, d_wk, d_wv, d_wo, d_lnw, d_lnb, d_bq, d_bk, d_bv, d_bo)
 

time: 144 us -> 136 us (0.944)
  local copies, waits for them, and re-layouts: 12.4 us -> 0.18 us
  Pallas kernels: 128 us -> 133 us
    unnamed x16 -> x0, local copies, waits for them, and re-layouts: 9.2 us -> none
    pallas_call x0 -> x1, Pallas kernels: none -> 7.37 us  [finish(): pl.pallas_call(functools.partial(finish_body, hd), grid_spec=pltpu.Prefet...]
    slice x2 -> x0, local copies, waits for them, and re-layouts: 3.02 us -> none  [the longest x1 1.62 us: device_fn(): d_lnw, d_lnb, d_bo, d_bq = (vec[n] for n in range(4))]
    pallas_call x1, Pallas kernels: 128 us -> 126 us  [mega(): pl.pallas_call(functools.partial(mega_body, nh, hd, tile, scale), in_spec...]
where the time goes in v4:
time: 136 us
  Pallas kernels  133 us (98%)
  other arithmetic  2.25 us (2%)
    pallas_call x1, Pallas kernels, mega(): pl.pallas_call(functools.partial(mega_body, nh, hd, tile, scale), in_spec...  126 us
    pallas_call x1, Pallas kernels, finish(): pl.pallas_call(functools.partial(finish_body, hd), grid_spec=pltpu.Prefet...  7.37 us

profile of v4, /device:TPU:0, one launch (start us, length us, event | category | flops | bytes accessed | tf_op | source)
XLA Modules:
  0.0 136.3 jit_solution(15431970726710960170)
XLA Ops:
  0.7 0.7 multiply_divide_fusion
  1.3 0.1 add_bitcast_fusion
  1.4 0.1 add_subtract_fusion
  1.5 0.1 copy.26
  1.6 0.1 mul.31
  1.7 0.6 fusion
  2.3 0.8 pad_maximum_fusion
  3.1 125.6 %sublayer.1 = (bf16[2,256,1536]{2,1,0:T(8,128)(2,1)}, bf16[2,256,1536]{2,1,0:T(8,128)(2,1)}, f32[384,1024]{1,0:T(8,128)}, f32[384,1024]{1,0:T(8,128)}, f32[384,1536]{1,0:T(8,128)}, /*index=5*/f32[8,1536]{1,0:T(8,128)}) custom-call(bf16[2,256,1536]{2,1,0:T(8,128)(2,1)} %bitcast.17, bf16[2,256,1536]{2,1,0:T(8,128)(2,1)} %bitcast.18, ...), custom_call_target="tpu_custom_call" | custom-call | tf_op jit(solution)/shard_map/sublayer/pallas_call | solution.py:528
  128.8 7.4 %finish.1 = (bf16[512,1536]{1,0:T(8,128)(2,1)}, bf16[512,1536]{1,0:T(8,128)(2,1)}, f32[384,1536]{1,0:T(8,128)}, f32[384,256]{1,0:T(8,128)}, f32[384,256]{1,0:T(8...) custom-call(s32[1]{0:T(128)} %bitcast.c_ref, ...), custom_call_target="tpu_custom_call" | custom-call | tf_op jit(solution)/shard_map/finish/pallas_call | solution.py:578
  (3 shorter events, 0.0 us)

commit v5 on v4

--- a/solution.py
+++ b/solution.py
@@ -31,12 +31,11 @@
 def rope_tables(starts, piece, long_factor):
     half_dim = long_factor.shape[0]
     exponent = jnp.arange(half_dim, dtype=F32) * (1.0 / half_dim)
-    inv_freq = 1.0 / (long_factor * THETA ** exponent)
+    inv_freq = jnp.tile(1.0 / (long_factor * THETA ** exponent), 2)
+    sign = jnp.where(jnp.arange(2 * half_dim) < half_dim, -1.0, 1.0)
     positions = jnp.concatenate([jnp.arange(piece, dtype=jnp.int32), starts])
     angle = positions.astype(F32)[:, None] * inv_freq[None, :]
-    cos_t = jnp.cos(angle)
-    sin_t = jnp.sin(angle)
-    return jnp.concatenate([cos_t, cos_t], axis=1), jnp.concatenate([-sin_t, sin_t], axis=1)
+    return jnp.cos(angle), jnp.sin(angle) * sign[None, :]
 
 
 def tile_tables(cos_ref, sin_ref, piece, t):
@@ -200,13 +199,14 @@
         f_e1.start()
         f_h0.start()
         f_d0.start()
-        n_d.wait_recv()
 
         def first_four(t, _):
             project(t, t)
             return _
 
-        lax.fori_loop(0, 4, first_four, 0)
+        lax.fori_loop(0, 2, first_four, 0)
+        n_d.wait_recv()
+        lax.fori_loop(2, 4, first_four, 0)
         lax.fori_loop(0, 4, turn, 0)
         DK[...] = jnp.zeros_like(DK)
         DV[...] = jnp.zeros_like(DV)
@@ -326,33 +326,30 @@
             sin_t = st.T[hd // 2:]
             for n in range(nh):
                 lanes = slice(n * tile, (n + 1) * tile)
-                o_t = OT[:, lanes].astype(BF16)
-                rows = slice((n % third) * hd, (n % third + 1) * hd)
-
-                @pl.when(jnp.logical_and(holds, core == n // third))
-                def _():
-                    AT[t, rows, :] = o_t
-
-                @pl.when(jnp.logical_and(holds, core != n // third))
-                def _():
-                    SEND[s % 2, rows, :] = o_t
-
                 gr = (DQT[:, lanes] * scale).astype(BF16).astype(F32)
                 a = gr[:hd // 2]
                 e = gr[hd // 2:]
                 gr = jnp.concatenate([a * cos_t + e * sin_t, e * cos_t - a * sin_t], axis=0).astype(BF16)
-                cols = slice(n * hd, (n + 1) * hd)
-                DQTT[cols, :] = gr
-
-                @pl.when(t // 2 == 0)
+                DQTT[s % 2, n * hd:(n + 1) * hd, :] = gr
+
+            for h in range(2):
+                @pl.when(jnp.logical_and(holds, core == h))
                 def _():
-                    ONA[t % 2, :, cols] = o_t.T
-                    DQA[t % 2, :, cols] = gr.T
-
-                @pl.when(t // 2 == 1)
+                    for n in range(nh):
+                        o_t = OT[:, n * tile:(n + 1) * tile].astype(BF16)
+                        rows = slice((n % third) * hd, (n % third + 1) * hd)
+                        if n // third == h:
+                            AT[t, rows, :] = o_t
+                        else:
+                            SEND[s % 2, rows, :] = o_t
+
+            for h, (o_out, q_out) in enumerate(((ONA, DQA), (ONS, DQS))):
+                @pl.when(t // 2 == h)
                 def _():
-                    ONS[t % 2, :, cols] = o_t.T
-                    DQS[t % 2, :, cols] = gr.T
+                    for n in range(nh):
+                        cols = slice(n * hd, (n + 1) * hd)
+                        o_out[t % 2, :, cols] = OT[:, n * tile:(n + 1) * tile].astype(BF16).T
+                        q_out[t % 2, :, cols] = DQTT[s % 2, cols, :].T
 
             @pl.when(holds)
             def _():
@@ -363,7 +360,11 @@
                 n_o.start()
                 n_q.start()
 
-            DWT[...] += dot(DQTT[...], H[t, :, lanes_of(chip, 2 * part)])
+            @pl.when(s % 2 == 1)
+            def _():
+                cols = lanes_of(chip, 2 * part)
+                DWT[...] += dot(DQTT[0], H[tile_at(s - 1), :, cols]) + dot(DQTT[1], H[t, :, cols])
+
             return same
 
         lax.fori_loop(0, 8, one_tile, 0)
@@ -372,7 +373,7 @@
                   pltpu.VMEM((4, nh, tile, hd), BF16), pltpu.VMEM((4, nh, tile, hd), BF16),
                   pltpu.VMEM((8, tile, tq), F32), pltpu.VMEM((8, tile, tq), BF16), pltpu.VMEM((8, 1, tq), F32),
                   pltpu.VMEM((2, tile, tq), BF16), pltpu.VMEM((2, tile, tq), BF16), pltpu.VMEM((hd, tq), F32), pltpu.VMEM((hd, tq), F32),
-                  pltpu.VMEM((qw, tile), BF16))
+                  pltpu.VMEM((2, qw, tile), BF16))
 
     def tail_phase(DWS, X, WQO, WOO, WKVO, DKVT, DWK, DWM, ACC, OUT, YB, XB):
         n_w = remote(DWS, DWR, ns, nr, 9, near)
@@ -407,13 +408,11 @@
         n_k.start()
         lax.fori_loop(4, 8, finish, 0)
 
-        DWK[...] = jnp.zeros_like(DWK)
-
-        def kv_grad(t, _):
-            DWK[...] += dot(DKVT[t], H[t, :, lanes_of(chip, 2 * part)])
-            return _
-
-        lax.fori_loop(0, 8, kv_grad, 0)
+        chip_cols = lanes_of(chip, 2 * part)
+        acc = dot(DKVT[0], H[0, :, chip_cols])
+        for t in range(1, 8):
+            acc += dot(DKVT[t], H[t, :, chip_cols])
+        DWK[...] = acc
         theirs = lanes_of(1 - core, part)
         mine = lanes_of(core, part)
         for cp in loads[:4]:
@@ -565,7 +564,7 @@
             r[...] = v_ref[n:n + 1, :r.shape[0]].reshape(r.shape[0])
 
 
-def finish(core, y, dx, mine, theirs, d_wo, vec, hd, kvw, steps=4):
+def finish(core, y, dx, mine, theirs, d_wo, vec, hd, kvw, steps=2):
     rows, width = y.shape
     part, cols = mine.shape
     qw = cols - 2 * hd

time: 136 us -> 131 us (0.963)
  Pallas kernels: 133 us -> 128 us
    pallas_call x1, Pallas kernels: 126 us -> 121 us  [mega(): pl.pallas_call(functools.partial(mega_body, nh, hd, tile, scale), in_spec...]
where the time goes in v5:
time: 131 us
  Pallas kernels  128 us (98%)
  other arithmetic  2.11 us (2%)
    pallas_call x1, Pallas kernels, mega(): pl.pallas_call(functools.partial(mega_body, nh, hd, tile, scale), in_spec...  121 us
    pallas_call x1, Pallas kernels, finish(): pl.pallas_call(functools.partial(finish_body, hd), grid_spec=pltpu.Prefet...  6.29 us

profile of v5, /device:TPU:0, one launch (start us, length us, event | category | flops | bytes accessed | tf_op | source)
XLA Modules:
  0.0 130.9 jit_solution(1986439038364633251)
XLA Ops:
  0.7 0.7 multiply_divide_fusion
  1.3 0.1 mul.46
  1.4 0.1 add_bitcast_fusion
  1.5 0.1 add_subtract_fusion
  1.6 0.1 copy.26
  1.7 0.1 mul.41
  1.8 1.3 fusion
  3.1 121.4 %sublayer.1 = (bf16[2,256,1536]{2,1,0:T(8,128)(2,1)}, bf16[2,256,1536]{2,1,0:T(8,128)(2,1)}, f32[384,1024]{1,0:T(8,128)}, f32[384,1024]{1,0:T(8,128)}, f32[384,1536]{1,0:T(8,128)}, /*index=5*/f32[8,1536]{1,0:T(8,128)}) custom-call(bf16[2,256,1536]{2,1,0:T(8,128)(2,1)} %bitcast.17, bf16[2,256,1536]{2,1,0:T(8,128)(2,1)} %bitcast.18, ...), custom_call_target="tpu_custom_call" | custom-call | tf_op jit(solution)/shard_map/sublayer/pallas_call | solution.py:527
  124.5 6.3 %finish.1 = (bf16[512,1536]{1,0:T(8,128)(2,1)}, bf16[512,1536]{1,0:T(8,128)(2,1)}, f32[384,1536]{1,0:T(8,128)}, f32[384,256]{1,0:T(8,128)}, f32[384,256]{1,0:T(8...) custom-call(s32[1]{0:T(128)} %bitcast.c_ref, ...), custom_call_target="tpu_custom_call" | custom-call | tf_op jit(solution)/shard_map/finish/pallas_call | solution.py:577
  (5 shorter events, 0.0 us)

commit v6 on v5

--- a/solution.py
+++ b/solution.py
@@ -100,8 +100,8 @@
     f_kv = remote(KV.at[0:2], KV.at[4:6], fs, fr, 0, far)
     f_kw = remote(KV.at[2:4], KV.at[6:8], fs, fr, 6, far)
     f_h1 = remote(H.at[1], H.at[5], fs, fr, 1, far)
-    f_d1 = remote(D.at[1, :tile // 2], D.at[5, :tile // 2], fs, fr, 2, far)
-    f_e1 = remote(D.at[1, tile // 2:], D.at[5, tile // 2:], fs, fr, 7, far)
+    f_d1 = remote(D.at[1, :tile // 4], D.at[5, :tile // 4], fs, fr, 2, far)
+    f_e1 = remote(D.at[1, tile // 4:], D.at[5, tile // 4:], fs, fr, 7, far)
     f_h0 = remote(H.at[0], H.at[4], fs, fr, 3, far)
     f_d0 = remote(D.at[0], D.at[4], fs, fr, 4, far)
     n_h5 = remote(H.at[5], H.at[7], ns, nr, 2, near)

time: 131 us -> 129 us (0.985)
  Pallas kernels: 128 us -> 126 us
    pallas_call x1, Pallas kernels: 121 us -> 120 us  [mega(): pl.pallas_call(functools.partial(mega_body, nh, hd, tile, scale), in_spec...]
where the time goes in v6:
time: 129 us
  Pallas kernels  126 us (98%)
  other arithmetic  2.11 us (2%)
    pallas_call x1, Pallas kernels, mega(): pl.pallas_call(functools.partial(mega_body, nh, hd, tile, scale), in_spec...  120 us
    pallas_call x1, Pallas kernels, finish(): pl.pallas_call(functools.partial(finish_body, hd), grid_spec=pltpu.Prefet...  6.29 us

profile of v6, /device:TPU:0, one launch (start us, length us, event | category | flops | bytes accessed | tf_op | source)
XLA Modules:
  0.0 129.2 jit_solution(16660288091160177677)
XLA Ops:
  0.7 0.7 multiply_divide_fusion
  1.3 0.1 mul.46
  1.4 0.1 add_bitcast_fusion
  1.5 0.1 add_subtract_fusion
  1.6 0.1 copy.26
  1.7 0.1 mul.41
  1.8 1.3 fusion
  3.1 119.7 %sublayer.1 = (bf16[2,256,1536]{2,1,0:T(8,128)(2,1)}, bf16[2,256,1536]{2,1,0:T(8,128)(2,1)}, f32[384,1024]{1,0:T(8,128)}, f32[384,1024]{1,0:T(8,128)}, f32[384,1536]{1,0:T(8,128)}, /*index=5*/f32[8,1536]{1,0:T(8,128)}) custom-call(bf16[2,256,1536]{2,1,0:T(8,128)(2,1)} %bitcast.17, bf16[2,256,1536]{2,1,0:T(8,128)(2,1)} %bitcast.18, ...), custom_call_target="tpu_custom_call" | custom-call | tf_op jit(solution)/shard_map/sublayer/pallas_call | solution.py:527
  122.8 6.3 %finish.1 = (bf16[512,1536]{1,0:T(8,128)(2,1)}, bf16[512,1536]{1,0:T(8,128)(2,1)}, f32[384,1536]{1,0:T(8,128)}, f32[384,256]{1,0:T(8,128)}, f32[384,256]{1,0:T(8...) custom-call(s32[1]{0:T(128)} %bitcast.c_ref, ...), custom_call_target="tpu_custom_call" | custom-call | tf_op jit(solution)/shard_map/finish/pallas_call | solution.py:577
  (5 shorter events, 0.0 us)
